TPU v7x, 256 devices: a whole 4x4x8 slice. The times are simulated.
256 devices in a mesh: dp: 8 (over x, y_lo), expert: 16 (over z, core), tensor: 2 (over y_hi).
Axes of the slice: x: 4, y: 4 (y_hi: 2, y_lo: 2; y = y_hi * 2 + y_lo), z: 8, core: 2. Of those that a mesh axis runs over, the one named last changes fastest.
Arguments:
- tokens: bfloat16 [1536, 256, 1280], P(('dp', 'expert', 'tensor')), may hold values from -16 to 16
- cotangent: bfloat16 [1536, 256, 1280], P(('dp', 'expert', 'tensor')), may hold values from -6 to 6
- norm_gain: float32 [1280], replicated, may hold values from 0.5 to 1.5
- slot_keys: bfloat16 [1280, 32], replicated, may hold values from -2 to 2
- w_in: bfloat16 [16, 1280, 2560], P('expert', None, 'tensor'), may hold values from -0.15625 to 0.15625
- w_out: bfloat16 [16, 2560, 1280], P('expert', 'tensor'), may hold values from -0.125 to 0.125
Outputs:
- grad_tokens: bfloat16 [1536, 256, 1280], P(('dp', 'expert', 'tensor'))
- grad_gain: float32 [1280], replicated
- grad_keys: float32 [1280, 32], replicated
- grad_in: bfloat16 [16, 1280, 2560], P('expert', 'dp', 'tensor')
- grad_out: bfloat16 [16, 2560, 1280], P('expert', 'tensor', 'dp')
All inputs are finite; a program needn't handle non-finite values.
Results may differ from a plain program's by a relative error of at most 0.014.
The roundings to bfloat16 on the way count: a program that leaves them out, or rounds other values in their place, can miss the bound.
Values may be sent and summed in bfloat16 or wider, within the bound.
No kernel may reach another device: no remote copies, remote signals or barrier semaphores. Data moves between devices by JAX's collectives and lax.ppermute only.
A program may use at most 128 MiB of HBM per device.

v0:
```python
import jax
import jax.numpy as jnp
from jax import lax
from jax.sharding import PartitionSpec as P

SLOT_PER = 2


EPSILON = 1e-06


def from_everyone(shard, axis):
    devices = lax.axis_size(axis)
    return lax.all_to_all(
        jnp.broadcast_to(shard[None], (devices, *shard.shape)), axis, 0, 0, tiled=True
    )


def in_order(tiles, dim):
    shape = list(tiles.shape[1:])
    shape[dim] *= tiles.shape[0]
    return jnp.moveaxis(tiles, 0, dim).reshape(shape)


def collect(shard, axis, dim):
    tiles = from_everyone(shard, axis)
    return in_order(tiles, dim)


def in_blocks(shard, dim, devices):
    before, after = (shard.shape[:dim], shard.shape[dim + 1 :])
    return jnp.moveaxis(shard.reshape(*before, devices, -1, *after), dim, 0)


def summed_on_arrival(shard, axis, dim):
    tiles = in_blocks(shard, dim, lax.axis_size(axis))
    arrived = lax.all_to_all(tiles, axis, split_axis=0, concat_axis=0, tiled=True)
    return arrived.sum(axis=0)


def sent_and_summed(shard, axis, dim):
    devices = lax.axis_size(axis)
    tiles = lax.all_to_all(in_blocks(shard, dim, devices), axis, 0, 0, tiled=True)
    return jnp.sum(tiles.astype(jnp.float32), axis=0)


def mixing_forward(tokens, gain, slot_keys):
    average = jnp.mean(tokens, axis=-1, keepdims=True, dtype=jnp.float32)
    centred = tokens.astype(jnp.float32) - average
    spread = jnp.mean(centred * centred, axis=-1, keepdims=True)
    inverse = lax.rsqrt(spread + EPSILON)
    scaled = centred * inverse
    normed = (scaled * gain).astype(jnp.bfloat16)
    logits = jnp.einsum("bmd,dn->bmn", normed, slot_keys, preferred_element_type=jnp.float32)
    dispatch = jax.nn.softmax(logits, axis=1)
    combine = jax.nn.softmax(logits, axis=2)
    dispatch_low = dispatch.astype(jnp.bfloat16)
    slot_values = jnp.einsum(
        "bmn,bmd->bnd", dispatch_low, normed, preferred_element_type=jnp.float32
    )
    return (slot_values, combine, (scaled, inverse, normed, dispatch, combine, dispatch_low))


def mixing_backward(saved, gain, slot_keys, slot_grad, combine_grad):
    scaled, inverse, normed, dispatch, combine, dispatch_low = saved
    grad_dispatch = jnp.einsum(
        "bnd,bmd->bmn", slot_grad, normed, preferred_element_type=jnp.float32
    )
    grad_normed = jnp.einsum(
        "bmn,bnd->bmd", dispatch_low, slot_grad, preferred_element_type=jnp.float32
    )
    grad_logits = dispatch * (
        grad_dispatch - jnp.sum(dispatch * grad_dispatch, axis=1, keepdims=True)
    )
    grad_logits = grad_logits + combine * (
        combine_grad - jnp.sum(combine * combine_grad, axis=2, keepdims=True)
    )
    keys_wide = slot_keys.astype(jnp.float32)
    grad_normed = grad_normed + jnp.einsum(
        "bmn,dn->bmd", grad_logits, keys_wide, precision=lax.Precision.HIGHEST
    )
    keys_term = jnp.einsum(
        "bmd,bmn->dn", normed.astype(jnp.float32), grad_logits, precision=lax.Precision.HIGHEST
    )
    gain_term = jnp.sum(grad_normed * scaled, axis=(0, 1))
    grad_scaled = grad_normed * gain
    first_mean = jnp.mean(grad_scaled, axis=-1, keepdims=True)
    second_mean = jnp.mean(grad_scaled * scaled, axis=-1, keepdims=True)
    grad_tok = inverse * (grad_scaled - first_mean - scaled * second_mean)
    return (grad_tok, gain_term, keys_term)


def contract_rows(left, right):
    return lax.dot_general(
        left, right, (((0,), (0,)), ((), ())), preferred_element_type=jnp.float32
    )


def contract_cols(left, right):
    return lax.dot_general(
        left, right, (((1,), (1,)), ((), ())), preferred_element_type=jnp.float32
    )


def local(tokens, cotangent, norm_gain, slot_keys, w_in, w_out):
    local_imgs, token_count, features = tokens.shape
    slot_count = slot_keys.shape[1]
    experts = slot_count // SLOT_PER
    slot_values, combine, saved = mixing_forward(tokens, norm_gain, slot_keys)
    slot_inputs = slot_values.astype(jnp.bfloat16).reshape(local_imgs, experts, SLOT_PER, features)
    arrived = lax.all_to_all(slot_inputs, "expert", split_axis=1, concat_axis=0, tiled=True)
    slot_rows = collect(arrived, "tensor", 0).reshape(-1, features)
    first_proj = w_in[0]
    second_proj = w_out[0]
    pre_act = jnp.dot(slot_rows, first_proj, preferred_element_type=jnp.float32)
    hidden = jax.nn.gelu(pre_act).astype(jnp.bfloat16)
    segment = hidden
    outputs = summed_on_arrival(
        jnp.dot(segment, second_proj, preferred_element_type=jnp.float32), "tensor", 0
    )
    outputs = outputs.astype(jnp.bfloat16).reshape(arrived.shape)
    returned = lax.all_to_all(outputs, "expert", split_axis=0, concat_axis=1, tiled=True).reshape(
        local_imgs, slot_count, features
    )
    combine_low = combine.astype(jnp.bfloat16)
    grad_slots = jnp.einsum(
        "bmn,bmd->bnd", combine_low, cotangent, preferred_element_type=jnp.float32
    )
    grad_slots = grad_slots.astype(jnp.bfloat16).reshape(local_imgs, experts, SLOT_PER, features)
    grad_combine = jnp.einsum(
        "bmd,bnd->bmn", cotangent, returned, preferred_element_type=jnp.float32
    )
    grads_sent = lax.all_to_all(grad_slots, "expert", split_axis=1, concat_axis=0, tiled=True)
    grad_rows = collect(grads_sent, "tensor", 0).reshape(-1, features)
    grad_hidden = contract_cols(grad_rows, second_proj)
    grad_pre = jax.vjp(jax.nn.gelu, pre_act)[1](grad_hidden)[0].astype(jnp.bfloat16)
    segment = grad_pre
    grad_in_rows = sent_and_summed(
        contract_cols(segment, first_proj).astype(jnp.bfloat16), "tensor", 0
    )
    grad_in_rows = grad_in_rows.astype(jnp.bfloat16).reshape(arrived.shape)
    grad_back = lax.all_to_all(
        grad_in_rows, "expert", split_axis=0, concat_axis=1, tiled=True
    ).reshape(local_imgs, slot_count, features)
    grad_tok, gain_term, keys_term = mixing_backward(
        saved, norm_gain, slot_keys, grad_back, grad_combine
    )
    grad_tokens = (cotangent.astype(jnp.float32) + grad_tok).astype(jnp.bfloat16)
    grad_gain, grad_keys = lax.psum((gain_term, keys_term), ("dp", "expert", "tensor"))
    columns = slot_rows
    grad_first = lax.psum_scatter(
        contract_rows(columns, grad_pre).astype(jnp.bfloat16), "dp", scatter_dimension=0, tiled=True
    )
    columns = grad_rows
    grad_second = (
        lax.psum_scatter(
            contract_rows(columns, hidden).astype(jnp.bfloat16),
            "dp",
            scatter_dimension=0,
            tiled=True,
        )
        .astype(jnp.float32)
        .T
    )
    return (
        grad_tokens,
        grad_gain,
        grad_keys,
        grad_first[None],
        grad_second.astype(jnp.bfloat16)[None],
    )


def solution(mesh):
    placed = (
        P(("dp", "expert", "tensor"), None, None),
        P(("dp", "expert", "tensor"), None, None),
        P(),
        P(),
        P("expert", None, "tensor"),
        P("expert", "tensor", None),
    )
    return jax.shard_map(
        local,
        mesh=mesh,
        in_specs=placed,
        out_specs=(
            P(("dp", "expert", "tensor"), None, None),
            P(),
            P(),
            P("expert", "dp", "tensor"),
            P("expert", "tensor", "dp"),
        ),
        check_vma=False,
    )
```

profile of v0, /device:TPU:1, one launch (start us, length us, event | category | flops | bytes accessed | tf_op | source)
XLA Modules:
  0.0 502.3 jit_solution(15583305845671244630)
XLA Ops:
  8.0 2.8 convert_reduce_fusion
  15.5 3.8 convolution_convert_fusion.3
  23.5 10.0 %all-to-all-start = ((bf16[6,16,2,1280]{3,2,0,1:T(2,128)(2,1)}), bf16[6,16,2,1280]{3,2,0,1:T(2,128)(2,1)}, u32[]{:S(2)}, u32[]{:S(2)}) async-start(bf16[6,16,2,1280]{3,2,0,1:T(2,128)(2,1)} %copy.15), calls=%async_computation | async-start | bytes 983040 | tf_op jit(solution)/shard_map/all_to_all | solution.py:133
  35.2 4.6 convolution_convert_fusion.2
  44.0 6.1 %all-to-all-done = bf16[6,16,2,1280]{3,2,0,1:T(2,128)(2,1)} async-done(((bf16[6,16,2,1280]{3,2,0,1:T(2,128)(2,1)}), bf16[6,16,2,1280]{3,2,0,1:T(2,128)(2,1)}, u32[]{:S(2)}, u32[]{:S(2)}) %all-to-all-start) | async-done | bytes 491552 | tf_op jit(solution)/shard_map/all_to_all | solution.py:133
  50.1 19.4 %all_to_all.80 = bf16[6,16,2,1280]{3,2,0,1:T(2,128)(2,1)S(1)} all-to-all(bf16[6,16,2,1280]{3,2,0,1:T(2,128)(2,1)} %copy.16), channel_id=1, replica_groups=mesh['dp'=8,'expert'=16,'tensor'=2] {'expert'}, dimensions={1} | all-to-all | bytes 983040 | tf_op jit(solution)/shard_map/all_to_all | solution.py:111
  70.0 18.9 %all_to_all.81 = bf16[2,96,1,2,1280]{4,3,2,1,0:T(2,128)(2,1)} all-to-all(bf16[2,96,1,2,1280]{4,3,2,1,0:T(2,128)(2,1)S(1)} %broadcast_in_dim.15), channel_id=1, replica_groups=mesh['dp'=8,'expert'=16,'tensor'=2] {'tensor'}, dimensions={0} | all-to-all | bytes 1966080 | tf_op jit(solution)/shard_map/all_to_all | solution.py:14
  91.4 4.6 all-to-all-start.1
  96.0 3.3 reshape_reshape.7
  99.3 4.4 multiply_convert_fusion
  103.7 6.3 %all-to-all-done.1 = bf16[2,96,1,2,1280]{4,3,2,1,0:T(2,128)(2,1)} async-done(((bf16[2,96,1,2,1280]{4,3,2,1,0:T(2,128)(2,1)}), bf16[2,96,1,2,1280]{4,3,2,1,0:T(2,128)(2,1)}, u32[]{:S(2)}, u32[]{:S(2)}) %all-to-all-start.1) | async-done | bytes 983072 | tf_op jit(solution)/shard_map/all_to_all | solution.py:14
  110.0 3.3 reshape_reshape.6
  113.3 4.9 fusion.33
  120.7 3.6 all-to-all-start.4
  124.2 4.9 fusion.16
  129.2 8.3 %all-to-all-done.4 = bf16[2,192,1280]{2,1,0:T(8,128)(2,1)S(1)} async-done(((bf16[2,192,1280]{2,1,0:T(8,128)(2,1)}), bf16[2,192,1280]{2,1,0:T(8,128)(2,1)S(1)}, u32[]{:S(2)}, u32[]{:S(2)}) %all-to-all-start.4) | async-done | bytes 983072 | tf_op jit(solution)/shard_map/all_to_all | solution.py:43
  137.5 3.7 all-to-all-start.6
  144.3 19.8 %all-to-all-done.6 = f32[2,192,1280]{2,1,0:T(8,128)S(1)} async-done(((f32[2,192,1280]{2,1,0:T(8,128)}), f32[2,192,1280]{2,1,0:T(8,128)S(1)}, u32[]{:S(2)}, u32[]{:S(2)}) %all-to-all-start.6) | async-done | bytes 1966112 | tf_op jit(solution)/shard_map/all_to_all | solution.py:37
  164.1 6.3 %all-to-all-start.5 = ((bf16[96,1,2,1280]{3,2,1,0:T(2,128)(2,1)}), bf16[96,1,2,1280]{3,2,1,0:T(2,128)(2,1)S(1)}, u32[]{:S(2)}, u32[]{:S(2)}) async-start(bf16[96,1,2,1280]{3,2,1,0:T(2,128)(2,1)} %reshape.82), calls=%async_computation.5 | async-start | bytes 983040 | tf_op jit(solution)/shard_map/all_to_all | solution.py:142
  171.5 15.6 %all-to-all-done.5 = bf16[96,1,2,1280]{3,2,1,0:T(2,128)(2,1)S(1)} async-done(((bf16[96,1,2,1280]{3,2,1,0:T(2,128)(2,1)}), bf16[96,1,2,1280]{3,2,1,0:T(2,128)(2,1)S(1)}, u32[]{:S(2)}, u32[]{:S(2)}) %all-to-all-start.5) | async-done | bytes 491552 | tf_op jit(solution)/shard_map/all_to_all | solution.py:142
  187.1 3.5 all-to-all-start.7
  191.4 3.5 multiply_reduce_fusion.2
  194.8 11.7 %all-to-all-done.7 = bf16[96,1,2,1280]{3,2,1,0:T(2,128)(2,1)S(1)} async-done(((bf16[96,1,2,1280]{3,2,1,0:T(2,128)(2,1)}), bf16[96,1,2,1280]{3,2,1,0:T(2,128)(2,1)S(1)}, u32[]{:S(2)}, u32[]{:S(2)}) %all-to-all-start.7) | async-done | bytes 491552 | tf_op jit(solution)/shard_map/all_to_all | solution.py:122
  207.0 3.5 multiply_reduce_fusion.1
  210.7 2.9 convolution_bitcast_fusion
  213.7 5.0 convolution_convert_fusion.1
  219.0 4.9 convolution_convert_fusion
  224.0 5.6 %fusion.44 = f32[6,256,1280]{2,1,0:T(8,128)} fusion(bf16[6,32,1280]{2,1,0:T(8,128)(2,1)S(1)} %reshape.83, f32[6,32]{1,0:T(8,128)S(1)} %get-tuple-element.8, f32[6,256,32]{1,2,0:T(8,128)} %copy-done.4), kind=kOutput, calls=%fused_computation.58 | convolution fusion | flops 125977024 | bytes 8553216 | tf_op jit(solution)/shard_map/bmn,bnd->bmd/dot_general | solution.py:69
  229.6 10.7 %fusion.14 = (f32[1280]{0:T(1024)S(1)}, f32[6,256]{1,0:T(8,128)S(1)}, f32[6,256]{1,0:T(8,128)S(1)}, f32[6,256,1280]{2,1,0:T(8,128)}) fusion(bf16[6,256,1280]{2,1,0:T(8,128)(2,1)} %param.6, f32[6,256]{1,0:T(8,128)S(1)} %add_rsqrt_fusion, f32[6,256]{1,0:T(8,128)S(1)} %broadcast_multiply_fusion.2, f32[1280]{0:T(1024)S(1)} %copy-done.10, ...), kind=kOutput, calls=%fused_computation.16 | convolution fusion | flops 774631168 | bytes 19974144 | tf_op jit(solution)/shard_map/bmn,dn->bmd/dot_general | solution.py:79
  240.2 79.7 %psum.14 = f32[1280]{0:T(1024)} all-reduce(f32[1280]{0:T(1024)S(1)} %get-tuple-element.5), channel_id=1, replica_groups=mesh['dp'=8,'expert'=16,'tensor'=2] {'dp','expert','tensor'}, use_global_device_ids=true, to_apply=%region_13.0 | all-reduce | flops 1280 | bytes 10240 | tf_op jit(solution)/shard_map/psum | solution.py:149
  319.9 8.7 %fusion.13 = bf16[6,256,1280]{2,1,0:T(8,128)(2,1)} fusion(bf16[6,256,1280]{2,1,0:T(8,128)(2,1)} %param.6, bf16[6,256,1280]{2,1,0:T(8,128)(2,1)} %param.7, f32[6,256,1280]{2,1,0:T(8,128)} %get-tuple-element.18, f32[6,256]{1,0:T(8,128)S(1)} %get-tuple-element.19, f32[6,256]{1,0:T(8,128)S(1)} %get-tuple-element.20, f32[1280]{0:T(1024)S(1)} %copy-done.10, ...), kind=kLoop, calls=%fused_computation.15 | loop fusion | flops 21626880 | bytes 19690496 | tf_op jit(solution)/shard_map/convert_element_type | solution.py:148
  328.6 164.7 %all-reduce.2.cloned.1.call-done = f32[1280,32]{0,1:T(8,128)} async-done(((f32[1280,32]{0,1:T(8,128)}), f32[1280,32]{0,1:T(8,128)}) %all-reduce.2.cloned.1.call-update) | async-done | bytes 163856 | tf_op jit(solution)/shard_map/psum | solution.py:149
  (56 shorter events, 27.8 us)
Async XLA Ops:
  8.0 91.3 %copy-start = (bf16[1,1280,1280]{2,1,0:T(8,128)(2,1)S(1)}, bf16[1,1280,1280]{2,1,0:T(8,128)(2,1)}, u32[]{:S(2)}) copy-start(bf16[1,1280,1280]{2,1,0:T(8,128)(2,1)} %param.10) | copy-start | bytes 9830404
  8.0 3.4 copy-start.2
  8.0 4.6 copy-start.10
  8.0 4.6 copy-start.8
  14.4 0.7 copy-start.4
  23.5 26.6 %all-to-all-start = ((bf16[6,16,2,1280]{3,2,0,1:T(2,128)(2,1)}), bf16[6,16,2,1280]{3,2,0,1:T(2,128)(2,1)}, u32[]{:S(2)}, u32[]{:S(2)}) async-start(bf16[6,16,2,1280]{3,2,0,1:T(2,128)(2,1)} %copy.15), calls=%async_computation | async-start | bytes 983040 | tf_op jit(solution)/shard_map/all_to_all | solution.py:133
  91.4 18.6 %all-to-all-start.1 = ((bf16[2,96,1,2,1280]{4,3,2,1,0:T(2,128)(2,1)}), bf16[2,96,1,2,1280]{4,3,2,1,0:T(2,128)(2,1)}, u32[]{:S(2)}, u32[]{:S(2)}) async-start(bf16[2,96,1,2,1280]{4,3,2,1,0:T(2,128)(2,1)} %broadcast_in_dim.13), calls=%async_computation.1 | async-start | bytes 1966080 | tf_op jit(solution)/shard_map/all_to_all | solution.py:14
  118.2 2.4 copy-start.11
  120.7 16.8 %all-to-all-start.4 = ((bf16[2,192,1280]{2,1,0:T(8,128)(2,1)}), bf16[2,192,1280]{2,1,0:T(8,128)(2,1)S(1)}, u32[]{:S(2)}, u32[]{:S(2)}) async-start(bf16[2,192,1280]{2,1,0:T(8,128)(2,1)} %bitcast.77), calls=%async_computation.4 | async-start | bytes 1966080 | tf_op jit(solution)/shard_map/all_to_all | solution.py:43
  137.5 26.6 %all-to-all-start.6 = ((f32[2,192,1280]{2,1,0:T(8,128)}), f32[2,192,1280]{2,1,0:T(8,128)S(1)}, u32[]{:S(2)}, u32[]{:S(2)}) async-start(f32[2,192,1280]{2,1,0:T(8,128)} %fusion.16), calls=%async_computation.6 | async-start | bytes 3932160 | tf_op jit(solution)/shard_map/all_to_all | solution.py:37
  144.3 47.1 %copy-start.7 = (f32[6,256,32]{1,2,0:T(8,128)S(1)}, f32[6,256,32]{1,2,0:T(8,128)}, u32[]{:S(2)}) copy-start(f32[6,256,32]{1,2,0:T(8,128)} %get-tuple-element.9) | copy-start | bytes 589828
  164.1 23.0 %all-to-all-start.5 = ((bf16[96,1,2,1280]{3,2,1,0:T(2,128)(2,1)}), bf16[96,1,2,1280]{3,2,1,0:T(2,128)(2,1)S(1)}, u32[]{:S(2)}, u32[]{:S(2)}) async-start(bf16[96,1,2,1280]{3,2,1,0:T(2,128)(2,1)} %reshape.82), calls=%async_computation.5 | async-start | bytes 983040 | tf_op jit(solution)/shard_map/all_to_all | solution.py:142
  187.1 19.4 %all-to-all-start.7 = ((bf16[96,1,2,1280]{3,2,1,0:T(2,128)(2,1)}), bf16[96,1,2,1280]{3,2,1,0:T(2,128)(2,1)S(1)}, u32[]{:S(2)}, u32[]{:S(2)}) async-start(bf16[96,1,2,1280]{3,2,1,0:T(2,128)(2,1)} %convert_element_type.73), calls=%async_computation.7 | async-start | bytes 983040 | tf_op jit(solution)/shard_map/all_to_all | solution.py:122
  190.5 302.7 %all-reduce.2.cloned.1.call-start = ((), (), s32[]{:S(2)}) async-start(), calls=%async_computation.10 | async-start | bytes 327680 | tf_op jit(solution)/shard_map/psum | solution.py:149
  207.0 3.7 copy-start.3
  210.7 3.0 copy-start.6
  213.6 5.4 %copy-start.5 = (bf16[384,1280]{1,0:T(8,128)(2,1)S(1)}, bf16[384,1280]{1,0:T(8,128)(2,1)}, u32[]{:S(2)}) copy-start(bf16[384,1280]{1,0:T(8,128)(2,1)} %reshape_reshape.6) | copy-start | bytes 2949124
  213.7 279.6 %reduce-scatter.3.cloned.1.call-start = ((), (), s32[]{:S(2)}) async-start(), calls=%async_computation.11 | async-start | bytes 3686400 | tf_op jit(solution)/shard_map/reduce_scatter | solution.py:151
  218.7 274.5 %reduce-scatter.5.cloned.1.call-start = ((), (), s32[]{:S(2)}) async-start(), calls=%async_computation.12 | async-start | bytes 3686400 | tf_op jit(solution)/shard_map/reduce_scatter | solution.py:156
  224.0 5.6 %copy-start.9 = (bf16[1280,32]{0,1:T(8,128)(2,1)S(1)}, bf16[1280,32]{0,1:T(8,128)(2,1)}, u32[]{:S(2)}) copy-start(bf16[1280,32]{0,1:T(8,128)(2,1)} %param.9) | copy-start | bytes 245764
  319.9 174.9 %copy-start.1 = (bf16[1,1280,1280]{2,1,0:T(8,128)(2,1)S(1)}, bf16[1,1280,1280]{2,1,0:T(8,128)(2,1)}, u32[]{:S(2)}) copy-start(bf16[1,1280,1280]{2,1,0:T(8,128)(2,1)} %param.10) | copy-start | bytes 9830404
Sparse Core Ops, SparseCore 0:
  213.8 279.4 all-reduce.1
Sparse Core Ops, SparseCore 1:
  218.8 71.0 reduce-scatter.2
  292.9 76.7 reduce-scatter.4
where the time goes:
time: 504 us; the launch traced here: 502 us
  waiting for transfers between devices  232 us (46%)
  blocking collectives  118 us (23%)
  matrix products  62.9 us (12%)
  starting transfers between devices  32.3 us (6%)
  local copies, waits for them, and re-layouts  24.8 us (5%)
  other arithmetic  16.2 us (3%)
  between operations  15.7 us (3%)
    psum x1, waiting for transfers between devices, local(): lax.psum((gain_term, keys_term), ('dp', 'expert', 'tensor'))  165 us
    psum x1, blocking collectives, local(): lax.psum((gain_term, keys_term), ('dp', 'expert', 'tensor'))  79.7 us
    all_to_all x1, waiting for transfers between devices, summed_on_arrival(): lax.all_to_all(tiles, axis, split_axis=0, concat_axis=0, tiled=True)  19.8 us
    all_to_all x1, blocking collectives, local(): lax.all_to_all(slot_inputs, 'expert', split_axis=1, concat_axis=0, tiled=...  19.4 us
    all_to_all x1, blocking collectives, from_everyone(): lax.all_to_all(jnp.broadcast_to(shard[None], (devices, *shard.shape)), ax...  18.9 us
    all_to_all x1, waiting for transfers between devices, local(): lax.all_to_all(grad_in_rows, 'expert', split_axis=0, concat_axis=1, tiled...  15.6 us
    all_to_all x1, waiting for transfers between devices, local(): lax.all_to_all(outputs, 'expert', split_axis=0, concat_axis=1, tiled=True)  11.7 us
    dot_general x1, matrix products, mixing_backward(): jnp.einsum('bmn,dn->bmd', grad_logits, keys_wide, precision=lax.Precision...  10.7 us
  transfers between devices with their start and end apart: 9, of which 7 were waited for; matrix products, arithmetic and copies ran while one was open for 13% of the time, Pallas kernels for 0%

commit v1 on v0

v1 whole, which is shorter than its diff:
```python
import jax
import jax.numpy as jnp
from jax import lax
from jax.sharding import PartitionSpec as P

SLOT_PER = 2


EPSILON = 1e-06

ROWS = 24
LANES = 128


def from_everyone(shard, axis):
    devices = lax.axis_size(axis)
    return lax.all_to_all(
        jnp.broadcast_to(shard[None], (devices, *shard.shape)), axis, 0, 0, tiled=True
    )


def swapped(value):
    return lax.ppermute(value, "tensor", [(0, 1), (1, 0)])


def mixing_forward(tokens, gain, slot_keys):
    average = jnp.mean(tokens, axis=-1, keepdims=True, dtype=jnp.float32)
    centred = tokens.astype(jnp.float32) - average
    spread = jnp.mean(centred * centred, axis=-1, keepdims=True)
    inverse = lax.rsqrt(spread + EPSILON)
    scaled = centred * inverse
    normed = (scaled * gain).astype(jnp.bfloat16)
    logits = jnp.einsum("bmd,dn->bmn", normed, slot_keys, preferred_element_type=jnp.float32)
    dispatch = jax.nn.softmax(logits, axis=1)
    combine = jax.nn.softmax(logits, axis=2)
    dispatch_low = dispatch.astype(jnp.bfloat16)
    slot_values = jnp.einsum(
        "bmn,bmd->bnd", dispatch_low, normed, preferred_element_type=jnp.float32
    )
    return (slot_values, combine, (scaled, inverse, normed, dispatch, combine, dispatch_low))


def split_wide(value):
    high = value.astype(jnp.bfloat16)
    low = (value - high.astype(jnp.float32)).astype(jnp.bfloat16)
    return high, low


def contract_rows(left, right):
    return lax.dot_general(
        left, right, (((0,), (0,)), ((), ())), preferred_element_type=jnp.float32
    )


def contract_cols(left, right):
    return lax.dot_general(
        left, right, (((1,), (1,)), ((), ())), preferred_element_type=jnp.float32
    )


def summed_everywhere(keys_term, gain_part):
    slots, features = keys_term.shape
    blocks = features // LANES
    group = lax.axis_size("expert")
    flat = jnp.concatenate(
        [
            keys_term.reshape(slots, blocks, LANES).transpose(1, 0, 2).reshape(-1, LANES),
            gain_part.reshape(blocks, LANES),
            jnp.zeros((group * ROWS - (slots + 1) * blocks, LANES), jnp.float32),
        ]
    ).reshape(group, ROWS, LANES)
    mine = jnp.sum(lax.all_to_all(flat, "expert", 0, 0, tiled=True), axis=0)
    mine = jnp.sum(from_everyone(mine, ("dp", "tensor")), axis=0)
    whole = from_everyone(mine, "expert").reshape(-1, LANES)
    keys_sum = whole[: slots * blocks].reshape(blocks, slots, LANES).transpose(1, 0, 2)
    return keys_sum.reshape(slots, features), whole[slots * blocks :][:blocks].reshape(-1)


def local(tokens, cotangent, norm_gain, slot_keys, w_in, w_out):
    local_imgs, token_count, features = tokens.shape
    slot_count = slot_keys.shape[1]
    experts = slot_count // SLOT_PER
    slot_values, combine, saved = mixing_forward(tokens, norm_gain, slot_keys)
    slot_low = slot_values.astype(jnp.bfloat16)
    slot_inputs = slot_low.reshape(local_imgs, experts, SLOT_PER, features)
    arrived = lax.all_to_all(slot_inputs, "expert", split_axis=1, concat_axis=0, tiled=True)
    own = arrived.reshape(-1, features)
    half = own.shape[0]
    slot_rows = jnp.concatenate([own, swapped(own)])
    combine_low = combine.astype(jnp.bfloat16)
    grad_slots = jnp.einsum(
        "bmn,bmd->bnd", combine_low, cotangent, preferred_element_type=jnp.float32
    )
    grad_slots = grad_slots.astype(jnp.bfloat16).reshape(local_imgs, experts, SLOT_PER, features)
    grads_sent = lax.all_to_all(grad_slots, "expert", split_axis=1, concat_axis=0, tiled=True)
    own_grads = grads_sent.reshape(-1, features)
    grad_rows = jnp.concatenate([own_grads, swapped(own_grads)])
    first_proj = w_in[0]
    second_proj = w_out[0]
    pre_act = jnp.dot(slot_rows, first_proj, preferred_element_type=jnp.float32)
    hidden = jax.nn.gelu(pre_act).astype(jnp.bfloat16)

    def reduced_and_returned(partial):
        theirs = swapped(partial[half:].astype(jnp.bfloat16))
        total = (partial[:half] + theirs.astype(jnp.float32)).astype(jnp.bfloat16)
        return lax.all_to_all(
            total.reshape(arrived.shape), "expert", split_axis=0, concat_axis=1, tiled=True
        ).reshape(local_imgs, slot_count, features)

    returned = reduced_and_returned(jnp.dot(hidden, second_proj, preferred_element_type=jnp.float32))
    grad_hidden = contract_cols(grad_rows, second_proj)
    grad_pre = jax.vjp(jax.nn.gelu, pre_act)[1](grad_hidden)[0].astype(jnp.bfloat16)
    grad_back = reduced_and_returned(contract_cols(grad_pre, first_proj))
    second_part = contract_rows(grad_rows, hidden).astype(jnp.bfloat16)
    first_part = contract_rows(slot_rows, grad_pre).astype(jnp.bfloat16)
    grad_second = lax.psum_scatter(second_part, "dp", scatter_dimension=0, tiled=True)
    grad_first = lax.psum_scatter(first_part, "dp", scatter_dimension=0, tiled=True)
    returned, grad_back, second_part, first_part = lax.optimization_barrier(
        (returned, grad_back, second_part, first_part)
    )

    scaled, inverse, normed, dispatch, combine, dispatch_low = saved
    combine_grad = jnp.einsum(
        "bmd,bnd->bmn", cotangent, returned, preferred_element_type=jnp.float32
    )
    grad_dispatch = jnp.einsum(
        "bnd,bmd->bmn", grad_back, normed, preferred_element_type=jnp.float32
    )
    grad_logits = dispatch * (
        grad_dispatch - jnp.sum(dispatch * grad_dispatch, axis=1, keepdims=True)
    )
    grad_logits = grad_logits + combine * (
        combine_grad - jnp.sum(combine * combine_grad, axis=2, keepdims=True)
    )
    high, low = split_wide(grad_logits)
    pair = jnp.concatenate([high, low], axis=2)
    keys_pair = jnp.einsum("bmn,bmd->nd", pair, normed, preferred_element_type=jnp.float32)
    keys_term = keys_pair[:slot_count] + keys_pair[slot_count:]
    gain_part = jnp.sum(grad_back.astype(jnp.float32) * slot_low.astype(jnp.float32), axis=(0, 1))
    keys_sum, gain_sum = summed_everywhere(keys_term, gain_part)
    keys_wide = slot_keys.astype(jnp.float32)
    grad_keys = keys_sum.T
    grad_gain = (gain_sum + jnp.sum(keys_wide * grad_keys, axis=1)) / norm_gain

    weights = jnp.concatenate([dispatch_low, pair], axis=2)
    keys_rows = jnp.broadcast_to(slot_keys.T[None], (local_imgs, slot_count, features))
    values = jnp.concatenate([grad_back, keys_rows, keys_rows], axis=1)
    grad_normed = jnp.einsum("bmn,bnd->bmd", weights, values, preferred_element_type=jnp.float32)
    grad_scaled = grad_normed * norm_gain
    first_mean = jnp.mean(grad_scaled, axis=-1, keepdims=True)
    second_mean = jnp.mean(grad_scaled * scaled, axis=-1, keepdims=True)
    grad_tok = inverse * (grad_scaled - first_mean - scaled * second_mean)
    grad_tokens = (cotangent.astype(jnp.float32) + grad_tok).astype(jnp.bfloat16)
    return (
        grad_tokens,
        grad_gain,
        grad_keys,
        grad_first[None],
        grad_second.T[None],
    )


def solution(mesh):
    placed = (
        P(("dp", "expert", "tensor"), None, None),
        P(("dp", "expert", "tensor"), None, None),
        P(),
        P(),
        P("expert", None, "tensor"),
        P("expert", "tensor", None),
    )
    return jax.shard_map(
        local,
        mesh=mesh,
        in_specs=placed,
        out_specs=(
            P(("dp", "expert", "tensor"), None, None),
            P(),
            P(),
            P("expert", "dp", "tensor"),
            P("expert", "tensor", "dp"),
        ),
        check_vma=False,
    )
```

time: 504 us -> 268 us (0.53)
  waiting for transfers between devices: 232 us -> 91.1 us
  blocking collectives: 118 us -> 0 us
  starting transfers between devices: 32.3 us -> 58.3 us
  matrix products: 62.9 us -> 39.8 us
  local copies, waits for them, and re-layouts: 24.8 us -> 36.9 us
  other arithmetic: 16.2 us -> 24.8 us
    psum x1 -> x0, waiting for transfers between devices: 165 us -> none  [local(): lax.psum((gain_term, keys_term), ('dp', 'expert', 'tensor'))]
    psum x1 -> x0, blocking collectives: 79.7 us -> none  [local(): lax.psum((gain_term, keys_term), ('dp', 'expert', 'tensor'))]
    ppermute x0 -> x4, waiting for transfers between devices: none -> 44.9 us  [swapped(): return lax.ppermute(value, 'tensor', [(0, 1), (1, 0)])]
    all_to_all x2 -> x0, blocking collectives: 38.3 us -> none  [the longest x1 19.4 us: local(): lax.all_to_all(slot_inputs, 'expert', split_axis=1, concat_axis=0, tiled=...]
    all_to_all x4, waiting for transfers between devices: 55.3 us -> 20.8 us  [the longest x2 11.7 us: reduced_and_returned(): lax.all_to_all(total.reshape(arrived.shape), 'expert', split_axis=0, conc...]
    dot_general x5 -> x4, matrix products: 27.6 us -> 12.7 us  [the longest x1 7.84 us: local(): jnp.einsum('bmn,bnd->bmd', weights, values, preferred_element_type=jnp.fl...]
    all_to_all x1 -> x2, starting transfers between devices: 4.58 us -> 17.4 us  [from_everyone(): lax.all_to_all(jnp.broadcast_to(shard[None], (devices, *shard.shape)), ax...]
    all_to_all x4, starting transfers between devices: 17.1 us -> 27.8 us  [the longest x2 14.4 us: reduced_and_returned(): lax.all_to_all(total.reshape(arrived.shape), 'expert', split_axis=0, conc...]
  transfers between devices with their start and end apart: 9 -> 13, of which waited for: 7 -> 10; matrix products, arithmetic and copies ran while one was open for 13% -> 29% of each run, Pallas kernels for 0% -> 0%
where the time goes in v1:
time: 268 us; the launch traced here: 265 us
  waiting for transfers between devices  91.1 us (34%)
  starting transfers between devices  58.3 us (22%)
  matrix products  39.8 us (15%)
  local copies, waits for them, and re-layouts  36.9 us (14%)
  other arithmetic  24.8 us (9%)
  between operations  14.5 us (5%)
    ppermute x4, waiting for transfers between devices, swapped(): return lax.ppermute(value, 'tensor', [(0, 1), (1, 0)])  44.9 us
    all_to_all x2, starting transfers between devices, from_everyone(): lax.all_to_all(jnp.broadcast_to(shard[None], (devices, *shard.shape)), ax...  17.4 us
    all_to_all x2, starting transfers between devices, reduced_and_returned(): lax.all_to_all(total.reshape(arrived.shape), 'expert', split_axis=0, conc...  14.4 us
    all_to_all x2, waiting for transfers between devices, reduced_and_returned(): lax.all_to_all(total.reshape(arrived.shape), 'expert', split_axis=0, conc...  11.7 us
    all_to_all x1, waiting for transfers between devices, local(): lax.all_to_all(grad_slots, 'expert', split_axis=1, concat_axis=0, tiled=T...  10.6 us
    all_to_all x1, starting transfers between devices, local(): lax.all_to_all(slot_inputs, 'expert', split_axis=1, concat_axis=0, tiled=...  9.97 us
    dot_general x2, matrix products, contract_rows(): lax.dot_general(left, right, (((0,), (0,)), ((), ())), preferred_element_...  9.41 us
    all_to_all x2, waiting for transfers between devices, from_everyone(): lax.all_to_all(jnp.broadcast_to(shard[None], (devices, *shard.shape)), ax...  9.07 us
  transfers between devices with their start and end apart: 13, of which 10 were waited for; matrix products, arithmetic and copies ran while one was open for 29% of the time, Pallas kernels for 0%

profile of v1, /device:TPU:1, one launch (start us, length us, event | category | flops | bytes accessed | tf_op | source)
XLA Modules:
  0.0 265.4 jit_solution(17931824056655264525)
XLA Ops:
  7.2 2.8 %convert_reduce_fusion = f32[6,256]{1,0:T(8,128)S(1)} fusion(bf16[6,256,1280]{2,1,0:T(8,128)(2,1)} %param.6), kind=kLoop, calls=%fused_computation.5 | loop fusion | flops 3930624 | bytes 3938304 | tf_op jit(solution)/shard_map/reduce_sum | solution.py:27
  16.0 2.4 convolution_convert_fusion.3
  20.4 2.2 copy.26
  22.6 10.0 %all-to-all-start = ((bf16[6,16,2,1280]{3,2,0,1:T(2,128)(2,1)}), bf16[6,16,2,1280]{3,2,0,1:T(2,128)(2,1)}, u32[]{:S(2)}, u32[]{:S(2)}) async-start(bf16[6,16,2,1280]{3,2,0,1:T(2,128)(2,1)} %copy.26), calls=%async_computation | async-start | bytes 983040 | tf_op jit(solution)/shard_map/all_to_all | solution.py:86
  33.3 3.6 %convolution_convert_fusion.2 = bf16[6,32,1280]{2,1,0:T(8,128)(2,1)} fusion(bf16[6,256,1280]{2,1,0:T(8,128)(2,1)} %param.7, f32[6,256]{1,0:T(8,128)S(1)} %get-tuple-element.17, f32[6,256,32]{1,2,0:T(8,128)S(1)} %fusion.61), kind=kOutput, calls=%fused_computation.31 | convolution fusion | flops 126223904 | bytes 4626432 | tf_op jit(solution)/shard_map/bmn,bmd->bnd/dot_general | solution.py:91
  38.9 2.2 copy.29
  41.0 8.2 %all-to-all-done = bf16[6,16,2,1280]{3,2,0,1:T(2,128)(2,1)} async-done(((bf16[6,16,2,1280]{3,2,0,1:T(2,128)(2,1)}), bf16[6,16,2,1280]{3,2,0,1:T(2,128)(2,1)}, u32[]{:S(2)}, u32[]{:S(2)}) %all-to-all-start) | async-done | bytes 491552 | tf_op jit(solution)/shard_map/all_to_all | solution.py:86
  49.2 4.1 %all-to-all-start.2 = ((bf16[6,16,2,1280]{3,2,0,1:T(2,128)(2,1)}), bf16[6,16,2,1280]{3,2,0,1:T(2,128)(2,1)}, u32[]{:S(2)}, u32[]{:S(2)}) async-start(bf16[6,16,2,1280]{3,2,0,1:T(2,128)(2,1)} %copy.29), calls=%async_computation.2 | async-start | bytes 983040 | tf_op jit(solution)/shard_map/all_to_all | solution.py:95
  55.3 2.9 %collective-permute-start = (bf16[192,1280]{1,0:T(8,128)(2,1)}, bf16[192,1280]{1,0:T(8,128)(2,1)}, u32[]{:S(2)}, u32[]{:S(2)}) collective-permute-start(bf16[192,1280]{1,0:T(8,128)(2,1)} %reshape.93), channel_id=1, source_target_pairs={{0,1},{1,0},{2,3},{3,2},{4,5},{5,4},{6,7},{7,6},{8,9},{9,8},{10,11... | collective-permute-start | bytes 1474568 | tf_op jit(solution)/shard_map/ppermute | solution.py:23
  58.3 10.6 %all-to-all-done.2 = bf16[6,16,2,1280]{3,2,0,1:T(2,128)(2,1)} async-done(((bf16[6,16,2,1280]{3,2,0,1:T(2,128)(2,1)}), bf16[6,16,2,1280]{3,2,0,1:T(2,128)(2,1)}, u32[]{:S(2)}, u32[]{:S(2)}) %all-to-all-start.2) | async-done | bytes 491552 | tf_op jit(solution)/shard_map/all_to_all | solution.py:95
  70.8 2.9 %collective-permute-start.2 = (bf16[192,1280]{1,0:T(8,128)(2,1)}, bf16[192,1280]{1,0:T(8,128)(2,1)S(1)}, u32[]{:S(2)}, u32[]{:S(2)}) collective-permute-start(bf16[192,1280]{1,0:T(8,128)(2,1)} %reshape.97), channel_id=1, source_target_pairs={{0,1},{1,0},{2,3},{3,2},{4,5},{5,4},{6,7},{7,6},{8,9},{9,8},{10,11... | collective-permute-start | bytes 1474568 | tf_op jit(solution)/shard_map/ppermute | solution.py:23
  78.4 6.5 %collective-permute-done.2 = bf16[192,1280]{1,0:T(8,128)(2,1)S(1)} collective-permute-done((bf16[192,1280]{1,0:T(8,128)(2,1)}, bf16[192,1280]{1,0:T(8,128)(2,1)S(1)}, u32[]{:S(2)}, u32[]{:S(2)}) %collective-permute-start.2) | collective-permute-done | bytes 491552 | tf_op jit(solution)/shard_map/ppermute | solution.py:23
  88.1 3.7 %convolution_convert_fusion = bf16[1280,1280]{1,0:T(8,128)(2,1)} fusion(bf16[384,1280]{1,0:T(8,128)(2,1)S(1)} %constant_dynamic-update-slice_fusion, bf16[384,1280]{1,0:T(8,128)(2,1)S(1)} %fusion.30), kind=kOutput, calls=%fused_computation.18 | convolution fusion | flops 1259929600 | bytes 5242880 | tf_op jit(solution)/shard_map/dot_general | solution.py:50
  91.8 2.8 %fusion.20 = f32[384,1280]{1,0:T(8,128)S(1)} fusion(bf16[384,1280]{1,0:T(8,128)(2,1)} %copy-done.19, bf16[1,1280,1280]{2,1,0:T(8,128)(2,1)S(1)} %copy-done), kind=kOutput, calls=%fused_computation.25 | convolution fusion | flops 1258291200 | bytes 6225920 | tf_op jit(solution)/shard_map/dot_general | solution.py:56
  94.7 3.0 %collective-permute-start.3 = (bf16[192,1280]{1,0:T(8,128)(2,1)S(1)}, bf16[192,1280]{1,0:T(8,128)(2,1)S(1)}, u32[]{:S(2)}, u32[]{:S(2)}) collective-permute-start(bf16[192,1280]{1,0:T(8,128)(2,1)S(1)} %slice.59), channel_id=1, source_target_pairs={{0,1},{1,0},{2,3},{3,2},{4,5},{5,4},{6,7},{7,6},{8,9},{9,8},{10,11... | collective-permute-start | bytes 1474568 | tf_op jit(solution)/shard_map/ppermute | solution.py:23
  101.7 22.5 %collective-permute-done.3 = bf16[192,1280]{1,0:T(8,128)(2,1)S(1)} collective-permute-done((bf16[192,1280]{1,0:T(8,128)(2,1)S(1)}, bf16[192,1280]{1,0:T(8,128)(2,1)S(1)}, u32[]{:S(2)}, u32[]{:S(2)}) %collective-permute-start.3) | collective-permute-done | bytes 491552 | tf_op jit(solution)/shard_map/ppermute | solution.py:23
  127.1 7.6 %all-to-all-start.3 = ((bf16[96,1,2,1280]{3,2,1,0:T(2,128)(2,1)}), bf16[96,1,2,1280]{3,2,1,0:T(2,128)(2,1)}, u32[]{:S(2)}, u32[]{:S(2)}) async-start(bf16[96,1,2,1280]{3,2,1,0:T(2,128)(2,1)} %bitcast.81), calls=%async_computation.3 | async-start | bytes 983040 | tf_op jit(solution)/shard_map/all_to_all | solution.py:106
  134.8 5.7 %convolution_convert_fusion.1 = bf16[1280,1280]{1,0:T(8,128)(2,1)} fusion(bf16[384,1280]{1,0:T(8,128)(2,1)} %copy-done.9, f32[384,1280]{1,0:T(8,128)} %copy-done.17), kind=kOutput, calls=%fused_computation.19 | convolution fusion | flops 1264353280 | bytes 6225920 | tf_op jit(solution)/shard_map/dot_general | solution.py:50
  140.5 15.9 %collective-permute-done.1 = bf16[192,1280]{1,0:T(8,128)(2,1)} collective-permute-done((bf16[192,1280]{1,0:T(8,128)(2,1)}, bf16[192,1280]{1,0:T(8,128)(2,1)}, u32[]{:S(2)}, u32[]{:S(2)}) %collective-permute-start.1) | collective-permute-done | bytes 491552 | tf_op jit(solution)/shard_map/ppermute | solution.py:23
  156.4 2.2 fusion.49
  160.5 6.8 %all-to-all-start.1 = ((bf16[96,1,2,1280]{3,2,1,0:T(2,128)(2,1)}), bf16[96,1,2,1280]{3,2,1,0:T(2,128)(2,1)}, u32[]{:S(2)}, u32[]{:S(2)}) async-start(bf16[96,1,2,1280]{3,2,1,0:T(2,128)(2,1)} %bitcast.82), calls=%async_computation.1 | async-start | bytes 983040 | tf_op jit(solution)/shard_map/all_to_all | solution.py:106
  168.0 2.2 copy.31
  172.1 11.7 %all-to-all-done.1 = bf16[96,1,2,1280]{3,2,1,0:T(2,128)(2,1)} async-done(((bf16[96,1,2,1280]{3,2,1,0:T(2,128)(2,1)}), bf16[96,1,2,1280]{3,2,1,0:T(2,128)(2,1)}, u32[]{:S(2)}, u32[]{:S(2)}) %all-to-all-start.1) | async-done | bytes 491552 | tf_op jit(solution)/shard_map/all_to_all | solution.py:106
  183.8 2.2 copy.28
  188.0 3.6 %convolution_bitcast_fusion.1 = f32[6,256,32]{1,2,0:T(8,128)S(1)} fusion(bf16[6,32,1280]{2,1,0:T(8,128)(2,1)} %reshape.95, bf16[6,256,1280]{2,1,0:T(8,128)(2,1)} %param.7), kind=kOutput, calls=%fused_computation.55 | convolution fusion | flops 125829120 | bytes 4620288 | tf_op jit(solution)/shard_map/bmd,bnd->bmn/dot_general | solution.py:123
  200.5 3.4 %all-to-all-start.4 = ((f32[16,24,128]{2,1,0:T(8,128)}), f32[16,24,128]{2,1,0:T(8,128)S(1)}, u32[]{:S(2)}, u32[]{:S(2)}) async-start(f32[16,24,128]{2,1,0:T(8,128)} %bitcast.84), calls=%async_computation.4 | async-start | bytes 393216 | tf_op jit(solution)/shard_map/all_to_all | solution.py:72
  204.9 7.8 %multiply_reduce_fusion = (f32[6,256]{1,0:T(8,128)S(1)}, f32[6,256]{1,0:T(8,128)S(1)}, f32[6,256,1280]{2,1,0:T(8,128)}) fusion(f32[1280]{0:T(1024)} %param.8, f32[6,256]{1,0:T(8,128)S(1)} %add_rsqrt_fusion, f32[6,256]{1,0:T(8,128)S(1)} %broadcast_multiply_fusion.2, bf16[6,256,1280]{2,1,0:T(8,128)(2,1)} %param.6, ...), kind=kOutput, calls=%fused_computation.20 | convolution fusion | flops 396555264 | bytes 13104128 | tf_op jit(solution)/shard_map/bmn,bnd->bmd/dot_general | solution.py:148
  214.5 10.1 %all-to-all-start.5 = ((f32[16,24,128]{2,1,0:T(8,128)}), f32[16,24,128]{2,1,0:T(8,128)S(1)}, u32[]{:S(2)}, u32[]{:S(2)}) async-start(f32[16,24,128]{2,1,0:T(8,128)} %broadcast_in_dim.14), calls=%async_computation.5 | async-start | bytes 393216 | tf_op jit(solution)/shard_map/all_to_all | solution.py:17
  225.2 7.4 %all-to-all-done.5 = f32[16,24,128]{2,1,0:T(8,128)S(1)} async-done(((f32[16,24,128]{2,1,0:T(8,128)}), f32[16,24,128]{2,1,0:T(8,128)S(1)}, u32[]{:S(2)}, u32[]{:S(2)}) %all-to-all-start.5) | async-done | bytes 196640 | tf_op jit(solution)/shard_map/all_to_all | solution.py:17
  233.3 7.3 %all-to-all-start.6 = ((f32[16,24,128]{2,1,0:T(8,128)}), f32[16,24,128]{2,1,0:T(8,128)S(1)}, u32[]{:S(2)}, u32[]{:S(2)}) async-start(f32[16,24,128]{2,1,0:T(8,128)} %broadcast_in_dim.15), calls=%async_computation.6 | async-start | bytes 393216 | tf_op jit(solution)/shard_map/all_to_all | solution.py:17
  240.6 8.5 %fusion.14 = bf16[6,256,1280]{2,1,0:T(8,128)(2,1)} fusion(bf16[6,256,1280]{2,1,0:T(8,128)(2,1)} %param.6, bf16[6,256,1280]{2,1,0:T(8,128)(2,1)} %param.7, f32[6,256,1280]{2,1,0:T(8,128)} %get-tuple-element.19, f32[6,256]{1,0:T(8,128)} %get-tuple-element.20, f32[6,256]{1,0:T(8,128)} %get-tuple-element.21, f32[1280]{0:T(1024)} %param.8, ...), kind=kLoop, calls=%fused_computation.16 | loop fusion | flops 21626880 | bytes 19690496 | tf_op jit(solution)/shard_map/convert_element_type | solution.py:153
  252.9 5.7 %reduce-scatter.5.cloned.1.call-done = bf16[160,1280]{1,0:T(8,128)(2,1)} async-done(((bf16[1280,1280]{1,0:T(8,128)(2,1)}), bf16[160,1280]{1,0:T(8,128)(2,1)}) %reduce-scatter.5.cloned.1.call-update) | async-done | bytes 409616 | tf_op jit(solution)/shard_map/reduce_scatter | solution.py:116
  (99 shorter events, 52.6 us)
Async XLA Ops:
  7.2 69.8 %copy-start = (bf16[1,1280,1280]{2,1,0:T(8,128)(2,1)S(1)}, bf16[1,1280,1280]{2,1,0:T(8,128)(2,1)}, u32[]{:S(2)}) copy-start(bf16[1,1280,1280]{2,1,0:T(8,128)(2,1)} %param.10) | copy-start | bytes 9830404
  7.2 3.4 %copy-start.1 = (bf16[6,256,1280]{2,1,0:T(8,128)(2,1)S(1)}, bf16[6,256,1280]{2,1,0:T(8,128)(2,1)}, u32[]{:S(2)}) copy-start(bf16[6,256,1280]{2,1,0:T(8,128)(2,1)} %param.6) | copy-start | bytes 11796484
  7.2 4.6 %copy-start.14 = (f32[1280]{0:T(1024)S(1)}, f32[1280]{0:T(1024)}, u32[]{:S(2)}) copy-start(f32[1280]{0:T(1024)} %param.8) | copy-start | bytes 15364
  7.2 4.6 %copy-start.7 = (bf16[1280,32]{0,1:T(8,128)(2,1)S(1)}, bf16[1280,32]{0,1:T(8,128)(2,1)}, u32[]{:S(2)}) copy-start(bf16[1280,32]{0,1:T(8,128)(2,1)} %param.9) | copy-start | bytes 245764
  10.6 194.3 %copy-start.12 = (f32[6,256]{1,0:T(8,128)}, f32[6,256]{1,0:T(8,128)S(1)}, u32[]{:S(2)}) copy-start(f32[6,256]{1,0:T(8,128)S(1)} %broadcast_multiply_fusion.2) | copy-start | bytes 18436
  11.8 193.1 %copy-start.13 = (f32[6,256]{1,0:T(8,128)}, f32[6,256]{1,0:T(8,128)S(1)}, u32[]{:S(2)}) copy-start(f32[6,256]{1,0:T(8,128)S(1)} %add_rsqrt_fusion) | copy-start | bytes 18436
  22.6 26.6 %all-to-all-start = ((bf16[6,16,2,1280]{3,2,0,1:T(2,128)(2,1)}), bf16[6,16,2,1280]{3,2,0,1:T(2,128)(2,1)}, u32[]{:S(2)}, u32[]{:S(2)}) async-start(bf16[6,16,2,1280]{3,2,0,1:T(2,128)(2,1)} %copy.26), calls=%async_computation | async-start | bytes 983040 | tf_op jit(solution)/shard_map/all_to_all | solution.py:86
  49.2 19.7 %all-to-all-start.2 = ((bf16[6,16,2,1280]{3,2,0,1:T(2,128)(2,1)}), bf16[6,16,2,1280]{3,2,0,1:T(2,128)(2,1)}, u32[]{:S(2)}, u32[]{:S(2)}) async-start(bf16[6,16,2,1280]{3,2,0,1:T(2,128)(2,1)} %copy.29), calls=%async_computation.2 | async-start | bytes 983040 | tf_op jit(solution)/shard_map/all_to_all | solution.py:95
  53.3 199.5 %reduce-scatter.3.cloned.1.call-start = ((), (), s32[]{:S(2)}) async-start(), calls=%async_computation.9 | async-start | bytes 3686400 | tf_op jit(solution)/shard_map/reduce_scatter | solution.py:117
  55.3 20.5 %collective-permute-start = (bf16[192,1280]{1,0:T(8,128)(2,1)}, bf16[192,1280]{1,0:T(8,128)(2,1)}, u32[]{:S(2)}, u32[]{:S(2)}) collective-permute-start(bf16[192,1280]{1,0:T(8,128)(2,1)} %reshape.93), channel_id=1, source_target_pairs={{0,1},{1,0},{2,3},{3,2},{4,5},{5,4},{6,7},{7,6},{8,9},{9,8},{10,11... | collective-permute-start | bytes 1474568 | tf_op jit(solution)/shard_map/ppermute | solution.py:23
  70.8 14.1 %collective-permute-start.2 = (bf16[192,1280]{1,0:T(8,128)(2,1)}, bf16[192,1280]{1,0:T(8,128)(2,1)S(1)}, u32[]{:S(2)}, u32[]{:S(2)}) collective-permute-start(bf16[192,1280]{1,0:T(8,128)(2,1)} %reshape.97), channel_id=1, source_target_pairs={{0,1},{1,0},{2,3},{3,2},{4,5},{5,4},{6,7},{7,6},{8,9},{9,8},{10,11... | collective-permute-start | bytes 1474568 | tf_op jit(solution)/shard_map/ppermute | solution.py:23
  77.0 8.0 %copy-start.15 = (bf16[1,1280,1280]{2,1,0:T(8,128)(2,1)S(1)}, bf16[1,1280,1280]{2,1,0:T(8,128)(2,1)}, u32[]{:S(2)}) copy-start(bf16[1,1280,1280]{2,1,0:T(8,128)(2,1)} %param.11) | copy-start | bytes 9830404
  78.4 8.6 %copy-start.17 = (f32[384,1280]{1,0:T(8,128)}, f32[384,1280]{1,0:T(8,128)S(1)}, u32[]{:S(2)}) copy-start(f32[384,1280]{1,0:T(8,128)S(1)} %fusion.22) | copy-start | bytes 5898244
  85.0 2.1 copy-start.9
  91.8 5.9 %copy-start.16 = (bf16[1,1280,1280]{2,1,0:T(8,128)(2,1)S(1)}, bf16[1,1280,1280]{2,1,0:T(8,128)(2,1)}, u32[]{:S(2)}) copy-start(bf16[1,1280,1280]{2,1,0:T(8,128)(2,1)} %param.11) | copy-start | bytes 9830404
  91.8 5.9 %copy-start.18 = (f32[384,1280]{1,0:T(8,128)S(1)}, f32[384,1280]{1,0:T(8,128)}, u32[]{:S(2)}) copy-start(f32[384,1280]{1,0:T(8,128)} %copy-done.17) | copy-start | bytes 5898244
  94.7 29.5 %collective-permute-start.3 = (bf16[192,1280]{1,0:T(8,128)(2,1)S(1)}, bf16[192,1280]{1,0:T(8,128)(2,1)S(1)}, u32[]{:S(2)}, u32[]{:S(2)}) collective-permute-start(bf16[192,1280]{1,0:T(8,128)(2,1)S(1)} %slice.59), channel_id=1, source_target_pairs={{0,1},{1,0},{2,3},{3,2},{4,5},{5,4},{6,7},{7,6},{8,9},{9,8},{10,11... | collective-permute-start | bytes 1474568 | tf_op jit(solution)/shard_map/ppermute | solution.py:23
  99.5 1.3 copy-start.4
  101.6 54.7 %collective-permute-start.1 = (bf16[192,1280]{1,0:T(8,128)(2,1)}, bf16[192,1280]{1,0:T(8,128)(2,1)}, u32[]{:S(2)}, u32[]{:S(2)}) collective-permute-start(bf16[192,1280]{1,0:T(8,128)(2,1)} %slice.60), channel_id=1, source_target_pairs={{0,1},{1,0},{2,3},{3,2},{4,5},{5,4},{6,7},{7,6},{8,9},{9,8},{10,11... | collective-permute-start | bytes 1474568 | tf_op jit(solution)/shard_map/ppermute | solution.py:23
  127.1 33.4 %all-to-all-start.3 = ((bf16[96,1,2,1280]{3,2,1,0:T(2,128)(2,1)}), bf16[96,1,2,1280]{3,2,1,0:T(2,128)(2,1)}, u32[]{:S(2)}, u32[]{:S(2)}) async-start(bf16[96,1,2,1280]{3,2,1,0:T(2,128)(2,1)} %bitcast.81), calls=%async_computation.3 | async-start | bytes 983040 | tf_op jit(solution)/shard_map/all_to_all | solution.py:106
  134.7 123.8 %reduce-scatter.5.cloned.1.call-start = ((), (), s32[]{:S(2)}) async-start(), calls=%async_computation.10 | async-start | bytes 3686400 | tf_op jit(solution)/shard_map/reduce_scatter | solution.py:116
  160.5 23.2 %all-to-all-start.1 = ((bf16[96,1,2,1280]{3,2,1,0:T(2,128)(2,1)}), bf16[96,1,2,1280]{3,2,1,0:T(2,128)(2,1)}, u32[]{:S(2)}, u32[]{:S(2)}) async-start(bf16[96,1,2,1280]{3,2,1,0:T(2,128)(2,1)} %bitcast.82), calls=%async_computation.1 | async-start | bytes 983040 | tf_op jit(solution)/shard_map/all_to_all | solution.py:106
  183.8 7.8 %copy-start.10 = (f32[6,256,32]{1,2,0:T(8,128)S(1)}, f32[6,256,32]{1,2,0:T(8,128)}, u32[]{:S(2)}) copy-start(f32[6,256,32]{1,2,0:T(8,128)} %get-tuple-element.18) | copy-start | bytes 589828
  188.0 4.0 %copy-start.2 = (bf16[6,256,1280]{2,1,0:T(8,128)(2,1)S(1)}, bf16[6,256,1280]{2,1,0:T(8,128)(2,1)}, u32[]{:S(2)}) copy-start(bf16[6,256,1280]{2,1,0:T(8,128)(2,1)} %param.6) | copy-start | bytes 11796484
  188.0 4.0 %copy-start.3 = (bf16[6,32,1280]{2,1,0:T(8,128)(2,1)S(1)}, bf16[6,32,1280]{2,1,0:T(8,128)(2,1)}, u32[]{:S(2)}) copy-start(bf16[6,32,1280]{2,1,0:T(8,128)(2,1)} %reshape.99) | copy-start | bytes 1474564
  192.0 1.5 copy-start.6
  194.4 1.6 copy-start.20
  194.5 1.6 copy-start.21
  200.5 13.3 %all-to-all-start.4 = ((f32[16,24,128]{2,1,0:T(8,128)}), f32[16,24,128]{2,1,0:T(8,128)S(1)}, u32[]{:S(2)}, u32[]{:S(2)}) async-start(f32[16,24,128]{2,1,0:T(8,128)} %bitcast.84), calls=%async_computation.4 | async-start | bytes 393216 | tf_op jit(solution)/shard_map/all_to_all | solution.py:72
  214.5 18.1 %all-to-all-start.5 = ((f32[16,24,128]{2,1,0:T(8,128)}), f32[16,24,128]{2,1,0:T(8,128)S(1)}, u32[]{:S(2)}, u32[]{:S(2)}) async-start(f32[16,24,128]{2,1,0:T(8,128)} %broadcast_in_dim.14), calls=%async_computation.5 | async-start | bytes 393216 | tf_op jit(solution)/shard_map/all_to_all | solution.py:17
  233.3 17.5 %all-to-all-start.6 = ((f32[16,24,128]{2,1,0:T(8,128)}), f32[16,24,128]{2,1,0:T(8,128)S(1)}, u32[]{:S(2)}, u32[]{:S(2)}) async-start(f32[16,24,128]{2,1,0:T(8,128)} %broadcast_in_dim.15), calls=%async_computation.6 | async-start | bytes 393216 | tf_op jit(solution)/shard_map/all_to_all | solution.py:17
  240.6 10.2 %copy-start.8 = (bf16[1280,32]{0,1:T(8,128)(2,1)S(1)}, bf16[1280,32]{0,1:T(8,128)(2,1)}, u32[]{:S(2)}) copy-start(bf16[1280,32]{0,1:T(8,128)(2,1)} %param.9) | copy-start | bytes 245764
  (3 other events, 2.3 us)
Sparse Core Ops, SparseCore 0:
  91.9 91.1 reduce-scatter.2
  186.2 72.3 reduce-scatter.4

commit v2 on v1

v2 whole, which is shorter than its diff:
```python
import jax
import jax.numpy as jnp
from jax import lax
from jax.experimental import pallas as pl
from jax.experimental.pallas import tpu as pltpu
from jax.sharding import PartitionSpec as P


SLOT_PER = 2


EPSILON = 1e-06


ROWS = 24
LANES = 128
CHUNK = 16
MIB = 1024 * 1024


def dot(left, right, dims):
    return lax.dot_general(left, right, (dims, ((), ())), preferred_element_type=jnp.float32)


NN = ((1,), (0,))
NT = ((1,), (1,))
TN = ((0,), (0,))


def from_everyone(shard, axis):
    devices = lax.axis_size(axis)
    return lax.all_to_all(
        jnp.broadcast_to(shard[None], (devices, *shard.shape)), axis, 0, 0, tiled=True
    )


def swapped(value):
    return lax.ppermute(value, "tensor", [(0, 1), (1, 0)])


def call(kernel, outs, ins, args, grid=None, scratch=(), flops=0, moved=0, limit=None):
    specs = {} if grid is None else {"grid": (grid,)}
    return pl.pallas_call(
        kernel,
        out_shape=[jax.ShapeDtypeStruct(s, d) for s, d, _ in outs],
        in_specs=list(ins),
        out_specs=[spec for _, _, spec in outs],
        scratch_shapes=list(scratch),
        compiler_params=pltpu.CompilerParams(vmem_limit_bytes=limit),
        cost_estimate=pl.CostEstimate(flops=flops, bytes_accessed=moved, transcendentals=0),
        **specs,
    )(*args)


def per_image(rows, cols):
    return pl.BlockSpec((1, rows, cols), lambda i: (i, 0, 0))


def whole(*shape):
    return pl.BlockSpec(shape, lambda i: (0,) * len(shape))


def packed_place(place, images):
    block = images * SLOT_PER
    place = place.astype(jnp.float32)
    expert = jnp.floor((place + 0.5) * (1.0 / (2 * block)))
    rest = place - expert * (2 * block)
    half = jnp.floor((rest + 0.5) * (1.0 / block))
    rest = rest - half * block
    image = jnp.floor((rest + 0.5) * (1.0 / SLOT_PER))
    return expert, half, image, rest - image * SLOT_PER


def selection(rows, images, half, by_image, packed_first):
    shape = (2 * rows, rows) if packed_first else (rows, 2 * rows)
    along = 0 if packed_first else 1
    thin = (2 * rows, 1) if packed_first else (1, 2 * rows)
    expert, part, image, slot = packed_place(lax.broadcasted_iota(jnp.int32, thin, along), images)
    if by_image:
        target = image * (rows // images) + expert * SLOT_PER + slot
    else:
        target = expert * (images * SLOT_PER) + image * SLOT_PER + slot
    target = jnp.where(part == half, target, -1.0)
    plain = lax.broadcasted_iota(jnp.int32, shape, 1 - along).astype(jnp.float32)
    return jnp.where(plain == target, 1.0, 0.0).astype(jnp.bfloat16)


def pack(value, images, by_image):
    rows, cols = value.shape
    total = 0.0
    for half in range(2):
        pick = selection(rows, images, half, by_image, True)
        total = total + dot(pick, value[:, half * (cols // 2) : (half + 1) * (cols // 2)], NN)
    return total.astype(jnp.bfloat16)


def unpack_into(out_ref, value, images, by_image):
    rows, cols = out_ref.shape
    for half in range(2):
        pick = selection(rows, images, half, by_image, False)
        out_ref[:, half * (cols // 2) : (half + 1) * (cols // 2)] = dot(pick, value, NN).astype(
            jnp.bfloat16
        )


def parts(wide, count):
    pieces = []
    for _ in range(count):
        piece = wide.astype(jnp.bfloat16)
        pieces.append(piece)
        wide = wide - piece.astype(jnp.float32)
    return pieces


def over_chunks(count, body):
    def group(g, carry):
        for part in range(4):
            body(pl.ds(pl.multiple_of((g * 4 + part) * CHUNK, CHUNK), CHUNK))
        return carry

    lax.fori_loop(0, count // (4 * CHUNK), group, 0)


def lane_blocks(features):
    return [slice(k * LANES, (k + 1) * LANES) for k in range(features // LANES)]


def softmax(logits, axis):
    exps = jnp.exp(logits - jnp.max(logits, axis=axis, keepdims=True))
    return exps / jnp.sum(exps, axis=axis, keepdims=True)


def started(copies):
    for copy in copies:
        copy.start()
    return copies


def copies_of(sources, targets, sems):
    return [
        pltpu.make_async_copy(source, target, sems.at[i])
        for i, (source, target) in enumerate(zip(sources, targets))
    ]


def forward_kernel(images, *refs):
    inputs, outputs, held = refs[:3], refs[3:10], refs[10:]
    tok, gain, keys, send, slots, normed, inverse, logs, disp, comb, mean, squares = held[:12]
    in_sems, small_sems, exit_sems, out_sems = held[12:]
    count, features = tok.shape[1:]
    slot_count = keys.shape[0]
    tokens_in = [inputs[0].at[i] for i in range(images)]
    arrivals = started(copies_of(tokens_in, [tok.at[i] for i in range(images)], in_sems))
    small_in = started(copies_of(inputs[1:], [gain, keys], small_sems))
    exits = copies_of(
        [normed.at[i] for i in range(images)], [outputs[2].at[i] for i in range(images)], exit_sems
    )
    results = copies_of(
        [send, slots, inverse, logs, disp, comb], outputs[:2] + outputs[3:], out_sems
    )
    ones = jnp.ones((features, LANES), jnp.bfloat16)
    for i in range(images):
        arrivals[i].wait()
        mean[i] = dot(tok[i], ones, NN) * (1.0 / features)

        def square(rows):
            middle = mean[i, rows, :]
            total = jnp.zeros_like(middle)
            for at in lane_blocks(features):
                centred = tok[i, rows, at].astype(jnp.float32) - middle
                total = total + centred * centred
            squares[i, rows, :] = total

        over_chunks(count, square)
    for i in range(images):
        spread = 0.0
        for piece in parts(squares[i], 3):
            spread = spread + dot(piece, ones[:LANES], NN)
        inverse[i] = lax.rsqrt(spread * (1.0 / features) + EPSILON)
    results[2].start()
    for copy in small_in:
        copy.wait()
    for i in range(images):

        def norm(rows):
            middle = mean[i, rows, :]
            scale = inverse[i, rows, :]
            for at in lane_blocks(features):
                centred = tok[i, rows, at].astype(jnp.float32) - middle
                normed[i, rows, at] = (centred * scale * gain[0:1, at]).astype(jnp.bfloat16)

        over_chunks(count, norm)
        exits[i].start()
        logs[i] = dot(keys[...], normed[i], NT)
    results[3].start()
    for i in range(images):
        disp[i] = softmax(logs[i], 1)
        comb[i] = softmax(logs[i], 0)
    results[4].start()
    results[5].start()
    for i in range(images):
        values = dot(disp[i].astype(jnp.bfloat16), normed[i], NN)
        slots[i * slot_count : (i + 1) * slot_count, :] = values.astype(jnp.bfloat16)
    results[1].start()
    send[...] = pack(slots[...], images, True)
    results[0].start()
    for copy in exits + results:
        copy.wait()


def grads_kernel(images, cot, comb, send, slots):
    i = pl.program_id(0)
    count = comb.shape[1]
    values = dot(comb[0].astype(jnp.bfloat16), cot[0], NN)
    slots[pl.ds(pl.multiple_of(i * count, count), count), :] = values.astype(jnp.bfloat16)

    @pl.when(i == images - 1)
    def _():
        send[...] = pack(slots[...], images, True)


def unpack_kernel(images, value, out):
    unpack_into(out, value[...], images, False)


def add_pack_kernel(images, own, other, out):
    total = (own[...] + other[...].astype(jnp.float32)).astype(jnp.bfloat16)
    out[...] = pack(total, images, False)


def combine_kernel(images, far_back, hbm, far_comb, out, back, cot, comb, slots, sems, small_sems):
    smalls = started(copies_of([far_back, far_comb], [back, comb], small_sems))
    per = [hbm.at[i] for i in range(images)]
    arrivals = started(copies_of(per, [cot.at[i] for i in range(images)], sems))
    for copy in smalls:
        copy.wait()
    unpack_into(slots, back[...], images, True)
    count = comb.shape[1]
    for i in range(images):
        arrivals[i].wait()
        grad = dot(slots[i * count : (i + 1) * count, :], cot[i], NT)
        weight = comb[i]
        out[i] = weight * (grad - jnp.sum(weight * grad, axis=0, keepdims=True))


def logits_kernel(images, *refs):
    inputs, (grads, pair, sums), held = refs[:8], refs[8:11], refs[11:]
    back, slots, normed, logs, disp, part, keys, gain, total, sems, small_sems = held
    targets = [back, logs, disp, part, keys, gain, slots]
    sources = [inputs[0]] + list(inputs[3:]) + [inputs[1]]
    smalls = started(copies_of(sources, targets, small_sems))
    per = [inputs[2].at[i] for i in range(images)]
    arrivals = started(copies_of(per, [normed.at[i] for i in range(images)], sems))
    smalls[0].wait()
    unpack_into(grads, back[...], images, True)
    for copy in smalls[1:]:
        copy.wait()
    count = disp.shape[1]
    tokens = normed.shape[1]
    share = 1.0 / normed.shape[2]
    keys_share = jnp.sum(keys[...].astype(jnp.float32) * gain[...], axis=1, keepdims=True)
    place = lax.broadcasted_iota(jnp.int32, (16, tokens), 0)
    for i in range(images):
        arrivals[i].wait()
        mine = grads[i * count : (i + 1) * count, :]
        grad = dot(mine, normed[i], NT)
        weight = disp[i]
        wide = weight * (grad - jnp.sum(weight * grad, axis=1, keepdims=True)) + part[i]
        high, rest = parts(wide, 2)
        pair[i, :count, :] = high
        pair[i, count : 2 * count, :] = rest
        update = dot(pair[i, : 2 * count, :], normed[i], NN)
        total[...] = update if i == 0 else total[...] + update
        used = high.astype(jnp.float32) + rest.astype(jnp.float32)
        spread = weight.astype(jnp.bfloat16).astype(jnp.float32)
        mine_share = jnp.sum(mine.astype(jnp.float32) * gain[...], axis=1, keepdims=True)
        first = jnp.sum(spread * mine_share + used * keys_share, axis=0, keepdims=True) * share
        second = jnp.sum(spread * grad + used * logs[i], axis=0, keepdims=True) * share
        rows = jnp.zeros((16, tokens), jnp.float32)
        for k, row in enumerate(parts(first, 2) + parts(second, 2)):
            rows = jnp.where(place == k, row.astype(jnp.float32), rows)
        pair[i, 2 * count :, :] = rows.astype(jnp.bfloat16)
    product = grads[...].astype(jnp.float32) * slots[...].astype(jnp.float32)
    moved = jnp.sum(product, axis=0, keepdims=True)
    blocks = moved.shape[1] // LANES
    sums[blocks * count :, :] = jnp.zeros((sums.shape[0] - blocks * count, LANES), jnp.float32)
    for k, at in enumerate(lane_blocks(moved.shape[1])):
        sums[k * count : (k + 1) * count, :] = total[:count, at] + total[count:, at]
        sums[blocks * count + k : blocks * count + k + 1, :] = moved[:, at]


def tokens_kernel(normed, cot, inverse, pair, disp, grads, keys, gain, out, wide, inside):
    count, features = normed.shape[1:]
    weights = jnp.concatenate([disp[0].astype(jnp.bfloat16), pair[0]], axis=0)
    extra = weights.shape[0] - 3 * keys.shape[0]
    values = jnp.concatenate(
        [grads[...], keys[...], keys[...], jnp.zeros((extra, features), jnp.bfloat16)], axis=0
    )
    inside[...] = 1.0 / gain[...]
    wide[:, :features] = dot(weights, values, TN)
    row = lax.broadcasted_iota(jnp.int32, (extra, 2 * LANES), 0)
    col = lax.broadcasted_iota(jnp.int32, (extra, 2 * LANES), 1)
    pick = jnp.where((row < 4) & ((row < 2) == (col < LANES)), 1.0, 0.0).astype(jnp.bfloat16)
    wide[:, features:] = dot(pair[0, 2 * keys.shape[0] :, :], pick, TN)

    def norm(rows):
        first = wide[rows, features : features + LANES]
        second = wide[rows, features + LANES :]
        scale = inverse[0, rows, :]
        for at in lane_blocks(features):
            scaled = normed[0, rows, at].astype(jnp.float32) * inside[:, at]
            result = scale * (wide[rows, at] * gain[:, at] - first - scaled * second)
            out[0, rows, at] = (cot[0, rows, at].astype(jnp.float32) + result).astype(jnp.bfloat16)

    over_chunks(count, norm)


def after(value, *others):
    return lax.optimization_barrier((value, others))[0]


def piece_of(pieces, index, axis=0):
    return lax.dynamic_index_in_dim(pieces, index, axis, keepdims=False)


def chip_pairs(step, size):
    return [(i, (i + 2 * step) % size) for i in range(size)]


def to_other_chips(pieces):
    size = lax.axis_size("dp")
    chips = size // 2
    at = lax.axis_index("dp") // 2
    arrived = [
        lax.ppermute(piece_of(pieces, (at + step) % chips), "dp", chip_pairs(step, size))
        for step in range(1, chips)
    ]
    return [piece_of(pieces, at)] + arrived


def to_neighbour(value):
    return lax.ppermute(value, "dp", [(i, i ^ 1) for i in range(lax.axis_size("dp"))])


def added(pieces):
    total = pieces[0].astype(jnp.float32)
    for piece in pieces[1:]:
        total = total + piece.astype(jnp.float32)
    return total


def local(tokens, cotangent, norm_gain, slot_keys, w_in, w_out):
    images, count, features = tokens.shape
    slot_count = slot_keys.shape[1]
    rows = images * slot_count
    group = slot_count // SLOT_PER
    half = features // 2
    bf16, f32 = jnp.bfloat16, jnp.float32
    keys = slot_keys.T
    gain = norm_gain.reshape(1, features)
    tall = per_image(count, features)
    thin = per_image(slot_count, count)
    packed = whole(2 * rows, half)
    small = 2 * rows * features * count

    def sent(value):
        shaped = value.reshape(group, -1, half)
        return lax.all_to_all(shaped, "expert", 0, 0, tiled=True).reshape(2 * rows, half)

    local_ref = pl.BlockSpec(memory_space=pltpu.VMEM)
    far_ref = pl.BlockSpec(memory_space=pl.ANY)
    stacked = pltpu.VMEM((images, count, features), bf16)
    kept = [
        ((2 * rows, half), bf16),
        ((rows, features), bf16),
        ((images, count, features), bf16),
        ((images, count, LANES), f32),
        ((images, slot_count, count), f32),
        ((images, slot_count, count), f32),
        ((images, slot_count, count), f32),
    ]
    send_slots, slots, normed, inverse, logits, dispatch, combine = call(
        lambda *refs: forward_kernel(images, *refs),
        [(shape, kind, far_ref) for shape, kind in kept],
        [far_ref] * 3,
        (tokens, gain, keys),
        scratch=[stacked, pltpu.VMEM((1, features), f32), pltpu.VMEM((slot_count, features), bf16)]
        + [pltpu.VMEM(shape, kind) for shape, kind in kept]
        + [pltpu.VMEM((images, count, LANES), f32)] * 2
        + [pltpu.SemaphoreType.DMA((n,)) for n in (images, 2, images, 6)],
        flops=20 * small,
        moved=4 * images * count * features,
    )
    (send_grads,) = call(
        lambda *refs: grads_kernel(images, *refs),
        [((2 * rows, half), bf16, packed)],
        [tall, thin],
        (cotangent, combine),
        grid=images,
        scratch=[pltpu.VMEM((rows, features), bf16)],
        flops=10 * small,
        moved=2 * images * count * features,
    )

    def unpacked(value):
        return call(
            lambda *refs: unpack_kernel(images, *refs),
            [((rows, features), bf16, pl.BlockSpec(memory_space=pltpu.VMEM))],
            [pl.BlockSpec(memory_space=pltpu.VMEM)],
            (value,),
            flops=4 * small,
            moved=4 * rows * features,
            limit=16 * MIB,
        )[0]

    def summed(own, other):
        return call(
            lambda *refs: add_pack_kernel(images, *refs),
            [((2 * rows, half), bf16, pl.BlockSpec(memory_space=pltpu.VMEM))],
            [pl.BlockSpec(memory_space=pltpu.VMEM)] * 2,
            (own, other),
            flops=4 * small,
            moved=8 * rows * features,
            limit=16 * MIB,
        )[0]

    arrived = sent(send_slots)
    own_rows = unpacked(arrived)
    their_rows = swapped(own_rows)
    arrived = sent(send_grads)
    own_grads = unpacked(arrived)
    their_grads = swapped(own_grads)
    first_proj = w_in[0]
    second_proj = w_out[0]
    own_pre = dot(own_rows, first_proj, NN)
    own_hidden = jax.nn.gelu(own_pre).astype(bf16)
    their_pre = dot(their_rows, first_proj, NN)
    their_hidden = jax.nn.gelu(their_pre).astype(bf16)
    their_part = dot(their_hidden, second_proj, NN).astype(bf16)
    sums_out = swapped(their_part)

    def before_gelu(pre, grads):
        return jax.vjp(jax.nn.gelu, pre)[1](dot(grads, second_proj, NT))[0].astype(bf16)

    own_grad_pre = before_gelu(own_pre, own_grads)
    their_grad_pre = before_gelu(their_pre, their_grads)
    their_part = dot(their_grad_pre, first_proj, NT).astype(bf16)
    sums_in = swapped(their_part)
    own_part = dot(own_hidden, second_proj, NN)
    to_send = summed(own_part, sums_out)
    returned = sent(to_send)

    slot_rows = jnp.concatenate([own_rows, their_rows])
    grad_rows = jnp.concatenate([own_grads, their_grads])
    hidden = jnp.concatenate([own_hidden, their_hidden])
    grad_pre = jnp.concatenate([own_grad_pre, their_grad_pre])
    chips = lax.axis_size("dp") // 2
    low = lax.axis_index("dp") % 2
    second_part = dot(grad_rows, hidden, TN).astype(bf16).reshape(chips, -1, features)
    second_pieces = to_other_chips(second_part)
    first_part = dot(slot_rows, grad_pre, TN).astype(bf16).reshape(chips, 2, -1, features)
    own_part = dot(own_grad_pre, first_proj, NT)
    to_send = summed(own_part, sums_in)
    grad_back = sent(to_send)
    first_sent = after(piece_of(first_part, 1 - low, 1), sums_in)
    first_other = to_neighbour(first_sent)
    first_own = piece_of(first_part, low, 1)

    (combine_part,) = call(
        lambda *refs: combine_kernel(images, *refs),
        [((images, slot_count, count), f32, local_ref)],
        [far_ref] * 3,
        (returned, cotangent, combine),
        scratch=[
            pltpu.VMEM((2 * rows, half), bf16),
            stacked,
            pltpu.VMEM((images, slot_count, count), f32),
            pltpu.VMEM((rows, features), bf16),
            pltpu.SemaphoreType.DMA((images,)),
            pltpu.SemaphoreType.DMA((2,)),
        ],
        flops=10 * small,
        moved=2 * images * count * features,
    )
    grads, pair, sums = call(
        lambda *refs: logits_kernel(images, *refs),
        [
            ((rows, features), bf16, local_ref),
            ((images, 2 * slot_count + 16, count), bf16, local_ref),
            ((group * ROWS, LANES), f32, local_ref),
        ],
        [far_ref] * 8,
        (grad_back, slots, normed, logits, dispatch, combine_part, keys, gain),
        scratch=[
            pltpu.VMEM((2 * rows, half), bf16),
            pltpu.VMEM((rows, features), bf16),
            stacked,
        ]
        + [pltpu.VMEM((images, slot_count, count), f32)] * 3
        + [
            pltpu.VMEM((slot_count, features), bf16),
            pltpu.VMEM((1, features), f32),
            pltpu.VMEM((2 * slot_count, features), f32),
            pltpu.SemaphoreType.DMA((images,)),
            pltpu.SemaphoreType.DMA((7,)),
        ],
        flops=15 * small,
        moved=2 * images * count * features,
    )
    mine = lax.all_to_all(sums.reshape(group, ROWS, LANES), "expert", 0, 0, tiled=True)
    mine = jnp.sum(mine, axis=0)
    mine_two = from_everyone(mine, ("dp", "tensor"))
    first_other = after(first_other, mine)
    first_half = added([first_own, first_other]).astype(bf16)
    first_pieces = to_other_chips(first_half)
    second_pieces = after(second_pieces, mine)
    second_total = added(second_pieces).reshape(2, -1, features)
    second_other = to_neighbour(piece_of(second_total, 1 - low).astype(bf16))
    mine = jnp.sum(mine_two, axis=0)
    total = from_everyone(mine, "expert").reshape(-1, LANES)
    first_pieces = after(first_pieces, mine)
    grad_first = added(first_pieces).astype(bf16)
    second_other = after(second_other, mine)
    grad_second = added([piece_of(second_total, low), second_other]).astype(bf16)
    blocks = features // LANES
    keys_sum = total[: slot_count * blocks].reshape(blocks, slot_count, LANES)
    keys_sum = keys_sum.transpose(1, 0, 2).reshape(slot_count, features)
    gain_sum = total[slot_count * blocks :][:blocks].reshape(-1)
    gain_sum = gain_sum + jnp.sum(keys.astype(f32) * keys_sum, axis=0)

    (grad_tokens,) = call(
        tokens_kernel,
        [((images, count, features), bf16, tall)],
        [
            tall,
            tall,
            per_image(count, LANES),
            per_image(2 * slot_count + 16, count),
            thin,
            pl.BlockSpec((slot_count, features), lambda i: (i, 0)),
            whole(slot_count, features),
            whole(1, features),
        ],
        (normed, cotangent, inverse, pair, dispatch, grads, keys, gain),
        grid=images,
        scratch=[pltpu.VMEM((count, features + 2 * LANES), f32), pltpu.VMEM((1, features), f32)],
        flops=20 * small,
        moved=6 * images * count * features,
    )
    return (
        grad_tokens,
        gain_sum / norm_gain,
        keys_sum.T,
        grad_first[None],
        grad_second.T[None],
    )


def solution(mesh):
    placed = (
        P(("dp", "expert", "tensor"), None, None),
        P(("dp", "expert", "tensor"), None, None),
        P(),
        P(),
        P("expert", None, "tensor"),
        P("expert", "tensor", None),
    )
    return jax.shard_map(
        local,
        mesh=mesh,
        in_specs=placed,
        out_specs=(
            P(("dp", "expert", "tensor"), None, None),
            P(),
            P(),
            P("expert", "dp", "tensor"),
            P("expert", "tensor", "dp"),
        ),
        check_vma=False,
    )
```

time: 268 us -> 216 us (0.81)
  Pallas kernels: 0 us -> 46.4 us
  waiting for transfers between devices: 91.1 us -> 56.8 us
  local copies, waits for them, and re-layouts: 36.9 us -> 15.2 us
  other arithmetic: 24.8 us -> 8.88 us
  matrix products: 39.8 us -> 24 us
  between operations: 14.5 us -> 0.97 us
  starting transfers between devices: 58.3 us -> 62.6 us
    pallas_call x0 -> x9, Pallas kernels: none -> 46.4 us  [call(): pl.pallas_call(kernel, out_shape=[jax.ShapeDtypeStruct(s, d) for s, d, _...]
    ppermute x4, waiting for transfers between devices: 44.9 us -> 16.6 us  [swapped(): return lax.ppermute(value, 'tensor', [(0, 1), (1, 0)])]
    reshape x11 -> x2, local copies, waits for them, and re-layouts: 21.2 us -> 2.12 us  [the longest x1 1.45 us: local(): gain = norm_gain.reshape(1, features)]
    dot_general x13 -> x10, matrix products: 39.8 us -> 24 us  [dot(): lax.dot_general(left, right, (dims, ((), ())), preferred_element_type=jnp...]
    ppermute x0 -> x8, starting transfers between devices: none -> 10.4 us  [the longest x6 7.74 us: to_other_chips(): lax.ppermute(piece_of(pieces, (at + step) % chips), 'dp', chip_pairs(step...]
    convert_element_type x4 -> x1, other arithmetic: 11.7 us -> 2.31 us  [local(): first_half = added([first_own, first_other]).astype(bf16)]
    all_to_all x2, starting transfers between devices: 17.4 us -> 8.68 us  [from_everyone(): lax.all_to_all(jnp.broadcast_to(shard[None], (devices, *shard.shape)), ax...]
    all_to_all x2, waiting for transfers between devices: 9.07 us -> 2.05 us  [from_everyone(): lax.all_to_all(jnp.broadcast_to(shard[None], (devices, *shard.shape)), ax...]
  transfers between devices with their start and end apart: 13 -> 19, of which waited for: 10 -> 8; matrix products, arithmetic and copies ran while one was open for 29% -> 18% of each run, Pallas kernels for 0% -> 16%
where the time goes in v2:
time: 216 us; the launch traced here: 215 us
  starting transfers between devices  62.6 us (29%)
  waiting for transfers between devices  56.8 us (26%)
  Pallas kernels  46.4 us (21%)
  matrix products  24 us (11%)
  local copies, waits for them, and re-layouts  15.2 us (7%)
  other arithmetic  8.88 us (4%)
    pallas_call x9, Pallas kernels, call(): pl.pallas_call(kernel, out_shape=[jax.ShapeDtypeStruct(s, d) for s, d, _...  46.4 us
    all_to_all x4, starting transfers between devices, sent(): lax.all_to_all(shaped, 'expert', 0, 0, tiled=True).reshape(2 * rows, half)  26.1 us
    dot_general x10, matrix products, dot(): lax.dot_general(left, right, (dims, ((), ())), preferred_element_type=jnp...  24 us
    all_to_all x4, waiting for transfers between devices, sent(): lax.all_to_all(shaped, 'expert', 0, 0, tiled=True).reshape(2 * rows, half)  21.4 us
    ppermute x4, waiting for transfers between devices, swapped(): return lax.ppermute(value, 'tensor', [(0, 1), (1, 0)])  16.6 us
    all_to_all x1, waiting for transfers between devices, local(): lax.all_to_all(sums.reshape(group, ROWS, LANES), 'expert', 0, 0, tiled=True)  10.2 us
    ppermute x4, starting transfers between devices, swapped(): return lax.ppermute(value, 'tensor', [(0, 1), (1, 0)])  9.09 us
    all_to_all x2, starting transfers between devices, from_everyone(): lax.all_to_all(jnp.broadcast_to(shard[None], (devices, *shard.shape)), ax...  8.68 us
  transfers between devices with their start and end apart: 19, of which 8 were waited for; matrix products, arithmetic and copies ran while one was open for 18% of the time, Pallas kernels for 16%

profile of v2, /device:TPU:1, one launch (start us, length us, event | category | flops | bytes accessed | tf_op | source)
XLA Modules:
  0.0 214.7 jit_solution(3360839221689226325)
XLA Ops:
  2.1 11.5 %shard_map.101 = (bf16[384,640]{1,0:T(8,128)(2,1)}, bf16[192,1280]{1,0:T(8,128)(2,1)}, bf16[6,256,1280]{2,1,0:T(8,128)(2,1)}, f32[6,256,128]{2,1,0:T(8,128)}, f3...) custom-call(bf16[6,256,1280]{2,1,0:T(8,128)(2,1)} %refs_0_.2, ...), custom_call_target="tpu_custom_call" | custom-call | flops 2516582400 | bytes 7864320 | tf_op jit(solution)/shard_map/pallas_call | solution.py:43
  13.6 10.0 %all-to-all-start.1 = ((bf16[16,24,640]{2,1,0:T(8,128)(2,1)}), bf16[16,24,640]{2,1,0:T(8,128)(2,1)}, u32[]{:S(2)}, u32[]{:S(2)}) async-start(bf16[16,24,640]{2,1,0:T(8,128)(2,1)} %bitcast.119), calls=%async_computation.1 | async-start | bytes 983040 | tf_op jit(solution)/shard_map/all_to_all | solution.py:368
  23.6 5.7 %shard_map.102 = bf16[384,640]{1,0:T(8,128)(2,1)} custom-call(bf16[6,256,1280]{2,1,0:T(8,128)(2,1)} %cot.1, f32[6,32,256]{2,1,0:T(8,128)} %get-tuple-element.28.refs_1_.refs_2_), custom_call_target="tpu_custom_call" | custom-call | flops 1258291200 | bytes 3932160 | tf_op jit(solution)/shard_map/pallas_call | solution.py:43
  29.3 11.0 %all-to-all-done.1 = bf16[16,24,640]{2,1,0:T(8,128)(2,1)} async-done(((bf16[16,24,640]{2,1,0:T(8,128)(2,1)}), bf16[16,24,640]{2,1,0:T(8,128)(2,1)}, u32[]{:S(2)}, u32[]{:S(2)}) %all-to-all-start.1) | async-done | bytes 491552 | tf_op jit(solution)/shard_map/all_to_all | solution.py:368
  40.2 4.1 %all-to-all-start = ((bf16[16,24,640]{2,1,0:T(8,128)(2,1)}), bf16[16,24,640]{2,1,0:T(8,128)(2,1)}, u32[]{:S(2)}, u32[]{:S(2)}) async-start(bf16[16,24,640]{2,1,0:T(8,128)(2,1)} %bitcast.118), calls=%async_computation | async-start | bytes 983040 | tf_op jit(solution)/shard_map/all_to_all | solution.py:368
  44.4 2.3 %shard_map.104 = bf16[192,1280]{1,0:T(8,128)(2,1)} custom-call(bf16[384,640]{1,0:T(8,128)(2,1)} %bitcast.5.refs_0_), custom_call_target="tpu_custom_call" | custom-call | flops 503316480 | bytes 983040 | tf_op jit(solution)/shard_map/pallas_call | solution.py:43
  46.6 2.9 %collective-permute-start.1 = (bf16[192,1280]{1,0:T(8,128)(2,1)}, bf16[192,1280]{1,0:T(8,128)(2,1)}, u32[]{:S(2)}, u32[]{:S(2)}) collective-permute-start(bf16[192,1280]{1,0:T(8,128)(2,1)} %shard_map.104), channel_id=1, source_target_pairs={{0,1},{1,0},{2,3},{3,2},{4,5},{5,4},{6,7},{7,6},{8,9},{9,8},{10,11... | collective-permute-start | bytes 1474568 | tf_op jit(solution)/shard_map/ppermute | solution.py:38
  49.5 10.4 %all-to-all-done = bf16[16,24,640]{2,1,0:T(8,128)(2,1)} async-done(((bf16[16,24,640]{2,1,0:T(8,128)(2,1)}), bf16[16,24,640]{2,1,0:T(8,128)(2,1)}, u32[]{:S(2)}, u32[]{:S(2)}) %all-to-all-start) | async-done | bytes 491552 | tf_op jit(solution)/shard_map/all_to_all | solution.py:368
  59.9 2.3 %shard_map.103 = bf16[192,1280]{1,0:T(8,128)(2,1)} custom-call(bf16[384,640]{1,0:T(8,128)(2,1)} %bitcast.2.refs_0_), custom_call_target="tpu_custom_call" | custom-call | flops 503316480 | bytes 983040 | tf_op jit(solution)/shard_map/pallas_call | solution.py:43
  62.2 2.9 %collective-permute-start = (bf16[192,1280]{1,0:T(8,128)(2,1)}, bf16[192,1280]{1,0:T(8,128)(2,1)}, u32[]{:S(2)}, u32[]{:S(2)}) collective-permute-start(bf16[192,1280]{1,0:T(8,128)(2,1)} %shard_map.103), channel_id=1, source_target_pairs={{0,1},{1,0},{2,3},{3,2},{4,5},{5,4},{6,7},{7,6},{8,9},{9,8},{10,11... | collective-permute-start | bytes 1474568 | tf_op jit(solution)/shard_map/ppermute | solution.py:38
  67.0 3.1 %multiply_convert_fusion = (bf16[192,1280]{1,0:T(8,128)(2,1)S(1)}, f32[192,1280]{1,0:T(8,128)}) fusion(bf16[192,1280]{1,0:T(8,128)(2,1)} %collective-permute-done.1, bf16[1,1280,1280]{2,1,0:T(8,128)(2,1)S(1)} %copy-done), kind=kOutput, calls=%fused_computation.54 | convolution fusion | flops 631357440 | bytes 5242880 | tf_op jit(solution)/shard_map/dot_general | solution.py:22
  72.1 3.3 %fusion.29 = bf16[192,1280]{1,0:T(8,128)(2,1)} fusion(f32[192,1280]{1,0:T(8,128)S(1)} %get-tuple-element.56, bf16[192,1280]{1,0:T(8,128)(2,1)} %shard_map.103, bf16[1,1280,1280]{2,1,0:T(8,128)(2,1)S(1)} %copy-done.3), kind=kOutput, calls=%fused_computation.34 | convolution fusion | flops 634060800 | bytes 5242880 | tf_op jit(solution)/shard_map/dot_general | solution.py:22
  75.4 11.4 %collective-permute-done.3.refs_1_ = bf16[192,1280]{1,0:T(8,128)(2,1)S(1)} collective-permute-done((bf16[192,1280]{1,0:T(8,128)(2,1)S(1)}, bf16[192,1280]{1,0:T(8,128)(2,1)S(1)}, u32[]{:S(2)}, u32[]{:S(2)}) %collective-permute-start.3) | collective-permute-done | bytes 491552 | tf_op jit(solution)/shard_map/ppermute | solution.py:38
  88.2 4.1 %all-to-all-start.3 = ((bf16[16,24,640]{2,1,0:T(8,128)(2,1)}), bf16[16,24,640]{2,1,0:T(8,128)(2,1)}, u32[]{:S(2)}, u32[]{:S(2)}) async-start(bf16[16,24,640]{2,1,0:T(8,128)(2,1)} %bitcast.108), calls=%async_computation.3 | async-start | bytes 983040 | tf_op jit(solution)/shard_map/all_to_all | solution.py:368
  92.3 3.7 %fusion.36 = bf16[192,1280]{1,0:T(8,128)(2,1)S(1)} fusion(f32[192,1280]{1,0:T(8,128)} %get-tuple-element.58, bf16[192,1280]{1,0:T(8,128)(2,1)} %collective-permute-done, bf16[1,1280,1280]{2,1,0:T(8,128)(2,1)} %param.11), kind=kOutput, calls=%fused_computation.41 | convolution fusion | flops 634060800 | bytes 5242880 | tf_op jit(solution)/shard_map/dot_general | solution.py:22
  97.3 3.0 %collective-permute-start.2 = (bf16[192,1280]{1,0:T(8,128)(2,1)S(1)}, bf16[192,1280]{1,0:T(8,128)(2,1)S(1)}, u32[]{:S(2)}, u32[]{:S(2)}) collective-permute-start(bf16[192,1280]{1,0:T(8,128)(2,1)S(1)} %fusion.20), channel_id=1, source_target_pairs={{0,1},{1,0},{2,3},{3,2},{4,5},{5,4},{6,7},{7,6},{8,9},{9,8},{10,11... | collective-permute-start | bytes 1474568 | tf_op jit(solution)/shard_map/ppermute | solution.py:38
  101.5 4.8 %convolution_convert_fusion = bf16[1280,1280]{1,0:T(8,128)(2,1)} fusion(bf16[192,1280]{1,0:T(8,128)(2,1)} %collective-permute-done, bf16[192,1280]{1,0:T(8,128)(2,1)} %shard_map.103, bf16[192,1280]{1,0:T(8,128)(2,1)S(1)} %copy-done.13, bf16[192,1280]{1,0:T(8,128)(2,1)S(1)} %copy-done.9), kind=kOutput, calls=%fused_computation | convolution fusion | flops 1263861760 | bytes 5242880 | tf_op jit(solution)/shard_map/dot_general | solution.py:22
  106.3 5.2 %collective-permute-done.2.refs_1_ = bf16[192,1280]{1,0:T(8,128)(2,1)S(1)} collective-permute-done((bf16[192,1280]{1,0:T(8,128)(2,1)S(1)}, bf16[192,1280]{1,0:T(8,128)(2,1)S(1)}, u32[]{:S(2)}, u32[]{:S(2)}) %collective-permute-start.2) | collective-permute-done | bytes 491552 | tf_op jit(solution)/shard_map/ppermute | solution.py:38
  112.9 7.8 %all-to-all-start.2 = ((bf16[16,24,640]{2,1,0:T(8,128)(2,1)}), bf16[16,24,640]{2,1,0:T(8,128)(2,1)}, u32[]{:S(2)}, u32[]{:S(2)}) async-start(bf16[16,24,640]{2,1,0:T(8,128)(2,1)} %bitcast.107), calls=%async_computation.2 | async-start | bytes 983040 | tf_op jit(solution)/shard_map/all_to_all | solution.py:368
  120.7 3.8 %dynamic-slice_bitcast_fusion.1 = (bf16[320,1280]{1,0:T(8,128)(2,1)}, bf16[320,1280]{1,0:T(8,128)(2,1)}, bf16[320,1280]{1,0:T(8,128)(2,1)}, bf16[320,1280]{1,0:T(8,128)(2,1)}) fusion(bf16[4,320,1280]{2,1,0:T(8,128)(2,1)} %bitcast.111, s32[]{:T(128)S(6)} %select_n.68, s32[]{:T(128)S(6)} %select_n.66, s32[]{:T(128)S(6)} %select_n.64, s32[]{:T(128)S(6)} %select_n.62), kind=kLoop, calls=%fused_computation.59 | loop fusion | bytes 6553616 | tf_op jit(solution)/shard_map/jit(dynamic_index_in_dim)/squeeze | solution.py:323
  125.7 2.4 %collective-permute-start.9 = (bf16[320,1280]{1,0:T(8,128)(2,1)}, bf16[320,1280]{1,0:T(8,128)(2,1)}, u32[]{:S(2)}, u32[]{:S(2)}) collective-permute-start(bf16[320,1280]{1,0:T(8,128)(2,1)} %get-tuple-element.48), channel_id=1, source_target_pairs={{0,128},{32,160},{64,192},{96,224},{128,0},{160,32},{192,64},{224,... | collective-permute-start | bytes 2457608 | tf_op jit(solution)/shard_map/ppermute | solution.py:335
  129.3 3.1 %convolution_convert_fusion.1 = bf16[1280,1280]{1,0:T(8,128)(2,1)S(1)} fusion(bf16[192,1280]{1,0:T(8,128)(2,1)} %collective-permute-done.1, bf16[192,1280]{1,0:T(8,128)(2,1)} %shard_map.104, bf16[192,1280]{1,0:T(8,128)(2,1)S(1)} %copy-done.11, bf16[192,1280]{1,0:T(8,128)(2,1)S(1)} %copy-done.7), kind=kOutput, calls=%fused_computation.1 | convolution fusion | flops 1263861760 | bytes 5242880 | tf_op jit(solution)/shard_map/dot_general | solution.py:22
  136.7 6.1 %shard_map.107.refs_5_ = f32[6,32,256]{2,1,0:T(8,128)} custom-call(bf16[384,640]{1,0:T(8,128)(2,1)} %bitcast.10.refs_0_, bf16[6,256,1280]{2,1,0:T(8,128)(2,1)} %cot.1, f32[6,32,256]{2,1,0:T(8,128)} %get-tuple-element.28.refs_1_.refs_2_), custom_call_target="tpu_custom_call" | custom-call | flops 1258291200 | bytes 3932160 | tf_op jit(solution)/shard_map/pallas_call | solution.py:43
  142.8 7.6 %shard_map.108 = (bf16[192,1280]{1,0:T(8,128)(2,1)}, bf16[6,80,256]{2,1,0:T(8,128)(2,1)}, f32[384,128]{1,0:T(8,128)}) custom-call(bf16[384,640]{1,0:T(8,128)(2,1)} %bitcast.8.refs_0_, bf16[192,1280]{1,0:T(8,128)(2,1)} %get-tuple-element.30.refs_1_, bf16[6,256,1280]{2,1,0:T(8,128)(2,1)} %get-tuple-element.26.refs_2_.normed, ...), custom_call_target="tpu_custom_call" | custom-call | flops 1887436800 | bytes 3932160 | tf_op jit(solution)/shard_map/pallas_call | solution.py:43
  150.4 8.4 %all-to-all-start.4 = ((f32[16,24,128]{2,1,0:T(8,128)}), f32[16,24,128]{2,1,0:T(8,128)S(1)}, u32[]{:S(2)}, u32[]{:S(2)}) async-start(f32[16,24,128]{2,1,0:T(8,128)} %bitcast.123), calls=%async_computation.4 | async-start | bytes 393216 | tf_op jit(solution)/shard_map/all_to_all | solution.py:510
  158.7 10.2 %all-to-all-done.4 = f32[16,24,128]{2,1,0:T(8,128)S(1)} async-done(((f32[16,24,128]{2,1,0:T(8,128)}), f32[16,24,128]{2,1,0:T(8,128)S(1)}, u32[]{:S(2)}, u32[]{:S(2)}) %all-to-all-start.4) | async-done | bytes 196640 | tf_op jit(solution)/shard_map/all_to_all | solution.py:510
  169.7 4.0 %all-to-all-start.5 = ((f32[16,24,128]{2,1,0:T(8,128)}), f32[16,24,128]{2,1,0:T(8,128)S(1)}, u32[]{:S(2)}, u32[]{:S(2)}) async-start(f32[16,24,128]{2,1,0:T(8,128)} %broadcast_in_dim.8), calls=%async_computation.5 | async-start | bytes 393216 | tf_op jit(solution)/shard_map/all_to_all | solution.py:32
  182.2 4.7 %all-to-all-start.6 = ((f32[16,24,128]{2,1,0:T(8,128)}), f32[16,24,128]{2,1,0:T(8,128)S(1)}, u32[]{:S(2)}, u32[]{:S(2)}) async-start(f32[16,24,128]{2,1,0:T(8,128)} %broadcast_in_dim.9), calls=%async_computation.6 | async-start | bytes 393216 | tf_op jit(solution)/shard_map/all_to_all | solution.py:32
  186.8 2.3 %fusion = bf16[4,160,1280]{2,1,0:T(8,128)(2,1)S(1)} fusion(bf16[4,160,1280]{2,1,0:T(8,128)(2,1)} %collective-permute-done.4, bf16[4,2,160,1280]{3,2,1,0:T(8,128)(2,1)} %bitcast.113, s32[]{:T(128)S(6)} %select_n.59), kind=kLoop, calls=%fused_computation.3 | loop fusion | flops 3276800 | bytes 4915204 | tf_op jit(solution)/shard_map/convert_element_type | solution.py:514
  193.3 9.8 %shard_map.109 = bf16[6,256,1280]{2,1,0:T(8,128)(2,1)} custom-call(bf16[6,256,1280]{2,1,0:T(8,128)(2,1)} %get-tuple-element.26.refs_2_.normed, bf16[6,256,1280]{2,1,0:T(8,128)(2,1)} %cot.1, f32[6,256,128]{2,1,0:T(8,128)} %get-tuple-element.27.inverse, bf16[6,80,256]{2,1,0:T(8,128)(2,1)} %get-tuple-element.33.pair, ...), custom_call_target="tpu_custom_call" | custom-call | flops 2516582400 | bytes 11796480 | tf_op jit(solution)/shard_map/pallas_call | solution.py:43
  205.2 6.2 %collective-permute-done.5 = bf16[160,1280]{1,0:T(8,128)(2,1)} collective-permute-done((bf16[160,1280]{1,0:T(8,128)(2,1)}, bf16[160,1280]{1,0:T(8,128)(2,1)}, u32[]{:S(2)}, u32[]{:S(2)}) %collective-permute-start.5) | collective-permute-done | bytes 409632 | tf_op jit(solution)/shard_map/ppermute | solution.py:335
  211.8 2.9 %fusion.54 = (bf16[1,160,1280]{2,1,0:T(8,128)(2,1)}, bf16[1,1280,160]{1,2,0:T(8,128)(2,1)}) fusion(bf16[160,1280]{1,0:T(8,128)(2,1)} %collective-permute-done.7, bf16[160,1280]{1,0:T(8,128)(2,1)} %collective-permute-done.6, bf16[160,1280]{1,0:T(8,128)(2,1)} %collective-permute-done.5, bf16[160,1280]{1,0:T(8,128)(2,1)} %get-tuple-element.38, ...), kind=kLoop, calls=%fused_computation.64 | loop fusion | flops 2252800 | bytes 3686404 | tf_op jit(solution)/shard_map/broadcast_in_dim | solution.py:554
  (71 shorter events, 32.9 us)
Async XLA Ops:
  0.6 64.4 %copy-start = (bf16[1,1280,1280]{2,1,0:T(8,128)(2,1)S(1)}, bf16[1,1280,1280]{2,1,0:T(8,128)(2,1)}, u32[]{:S(2)}) copy-start(bf16[1,1280,1280]{2,1,0:T(8,128)(2,1)} %param.10) | copy-start | bytes 9830404
  13.6 26.6 %all-to-all-start.1 = ((bf16[16,24,640]{2,1,0:T(8,128)(2,1)}), bf16[16,24,640]{2,1,0:T(8,128)(2,1)}, u32[]{:S(2)}, u32[]{:S(2)}) async-start(bf16[16,24,640]{2,1,0:T(8,128)(2,1)} %bitcast.119), calls=%async_computation.1 | async-start | bytes 983040 | tf_op jit(solution)/shard_map/all_to_all | solution.py:368
  40.2 19.7 %all-to-all-start = ((bf16[16,24,640]{2,1,0:T(8,128)(2,1)}), bf16[16,24,640]{2,1,0:T(8,128)(2,1)}, u32[]{:S(2)}, u32[]{:S(2)}) async-start(bf16[16,24,640]{2,1,0:T(8,128)(2,1)} %bitcast.118), calls=%async_computation | async-start | bytes 983040 | tf_op jit(solution)/shard_map/all_to_all | solution.py:368
  46.6 20.4 %collective-permute-start.1 = (bf16[192,1280]{1,0:T(8,128)(2,1)}, bf16[192,1280]{1,0:T(8,128)(2,1)}, u32[]{:S(2)}, u32[]{:S(2)}) collective-permute-start(bf16[192,1280]{1,0:T(8,128)(2,1)} %shard_map.104), channel_id=1, source_target_pairs={{0,1},{1,0},{2,3},{3,2},{4,5},{5,4},{6,7},{7,6},{8,9},{9,8},{10,11... | collective-permute-start | bytes 1474568 | tf_op jit(solution)/shard_map/ppermute | solution.py:38
  62.2 30.1 %collective-permute-start = (bf16[192,1280]{1,0:T(8,128)(2,1)}, bf16[192,1280]{1,0:T(8,128)(2,1)}, u32[]{:S(2)}, u32[]{:S(2)}) collective-permute-start(bf16[192,1280]{1,0:T(8,128)(2,1)} %shard_map.103), channel_id=1, source_target_pairs={{0,1},{1,0},{2,3},{3,2},{4,5},{5,4},{6,7},{7,6},{8,9},{9,8},{10,11... | collective-permute-start | bytes 1474568 | tf_op jit(solution)/shard_map/ppermute | solution.py:38
  67.0 4.3 %copy-start.8 = (bf16[192,1280]{1,0:T(8,128)(2,1)}, bf16[192,1280]{1,0:T(8,128)(2,1)S(1)}, u32[]{:S(2)}) copy-start(bf16[192,1280]{1,0:T(8,128)(2,1)S(1)} %get-tuple-element.55) | copy-start | bytes 1474564
  67.0 3.1 %copy-start.3 = (bf16[1,1280,1280]{2,1,0:T(8,128)(2,1)S(1)}, bf16[1,1280,1280]{2,1,0:T(8,128)(2,1)}, u32[]{:S(2)}) copy-start(bf16[1,1280,1280]{2,1,0:T(8,128)(2,1)} %param.11) | copy-start | bytes 9830404
  70.1 2.0 copy-start.12
  70.9 15.9 %collective-permute-start.3 = (bf16[192,1280]{1,0:T(8,128)(2,1)S(1)}, bf16[192,1280]{1,0:T(8,128)(2,1)S(1)}, u32[]{:S(2)}, u32[]{:S(2)}) collective-permute-start(bf16[192,1280]{1,0:T(8,128)(2,1)S(1)} %fusion.17), channel_id=1, source_target_pairs={{0,1},{1,0},{2,3},{3,2},{4,5},{5,4},{6,7},{7,6},{8,9},{9,8},{10,11... | collective-permute-start | bytes 1474568 | tf_op jit(solution)/shard_map/ppermute | solution.py:38
  88.2 24.8 %all-to-all-start.3 = ((bf16[16,24,640]{2,1,0:T(8,128)(2,1)}), bf16[16,24,640]{2,1,0:T(8,128)(2,1)}, u32[]{:S(2)}, u32[]{:S(2)}) async-start(bf16[16,24,640]{2,1,0:T(8,128)(2,1)} %bitcast.108), calls=%async_computation.3 | async-start | bytes 983040 | tf_op jit(solution)/shard_map/all_to_all | solution.py:368
  96.0 1.3 copy-start.10
  96.0 4.2 %copy-start.6 = (bf16[192,1280]{1,0:T(8,128)(2,1)S(1)}, bf16[192,1280]{1,0:T(8,128)(2,1)}, u32[]{:S(2)}) copy-start(bf16[192,1280]{1,0:T(8,128)(2,1)} %fusion.29) | copy-start | bytes 1474564
  97.3 4.2 %copy-start.9 = (bf16[192,1280]{1,0:T(8,128)(2,1)S(1)}, bf16[192,1280]{1,0:T(8,128)(2,1)}, u32[]{:S(2)}) copy-start(bf16[192,1280]{1,0:T(8,128)(2,1)} %copy-done.8) | copy-start | bytes 1474564
  97.3 4.2 %copy-start.13 = (bf16[192,1280]{1,0:T(8,128)(2,1)S(1)}, bf16[192,1280]{1,0:T(8,128)(2,1)}, u32[]{:S(2)}) copy-start(bf16[192,1280]{1,0:T(8,128)(2,1)} %copy-done.12) | copy-start | bytes 1474564
  97.3 14.2 %collective-permute-start.2 = (bf16[192,1280]{1,0:T(8,128)(2,1)S(1)}, bf16[192,1280]{1,0:T(8,128)(2,1)S(1)}, u32[]{:S(2)}, u32[]{:S(2)}) collective-permute-start(bf16[192,1280]{1,0:T(8,128)(2,1)S(1)} %fusion.20), channel_id=1, source_target_pairs={{0,1},{1,0},{2,3},{3,2},{4,5},{5,4},{6,7},{7,6},{8,9},{9,8},{10,11... | collective-permute-start | bytes 1474568 | tf_op jit(solution)/shard_map/ppermute | solution.py:38
  112.9 29.9 %all-to-all-start.2 = ((bf16[16,24,640]{2,1,0:T(8,128)(2,1)}), bf16[16,24,640]{2,1,0:T(8,128)(2,1)}, u32[]{:S(2)}, u32[]{:S(2)}) async-start(bf16[16,24,640]{2,1,0:T(8,128)(2,1)} %bitcast.107), calls=%async_computation.2 | async-start | bytes 983040 | tf_op jit(solution)/shard_map/all_to_all | solution.py:368
  120.7 8.6 %copy-start.7 = (bf16[192,1280]{1,0:T(8,128)(2,1)S(1)}, bf16[192,1280]{1,0:T(8,128)(2,1)}, u32[]{:S(2)}) copy-start(bf16[192,1280]{1,0:T(8,128)(2,1)} %fusion.29) | copy-start | bytes 1474564
  120.7 8.6 %copy-start.11 = (bf16[192,1280]{1,0:T(8,128)(2,1)S(1)}, bf16[192,1280]{1,0:T(8,128)(2,1)}, u32[]{:S(2)}) copy-start(bf16[192,1280]{1,0:T(8,128)(2,1)} %copy-done.10) | copy-start | bytes 1474564
  124.5 49.2 %collective-permute-start.8 = (bf16[320,1280]{1,0:T(8,128)(2,1)}, bf16[320,1280]{1,0:T(8,128)(2,1)}, u32[]{:S(2)}, u32[]{:S(2)}) collective-permute-start(bf16[320,1280]{1,0:T(8,128)(2,1)} %get-tuple-element.49), channel_id=1, source_target_pairs={{0,64},{32,96},{64,128},{96,160},{128,192},{160,224},{192,0},{224,... | collective-permute-start | bytes 2457608 | tf_op jit(solution)/shard_map/ppermute | solution.py:335
  125.7 48.0 %collective-permute-start.9 = (bf16[320,1280]{1,0:T(8,128)(2,1)}, bf16[320,1280]{1,0:T(8,128)(2,1)}, u32[]{:S(2)}, u32[]{:S(2)}) collective-permute-start(bf16[320,1280]{1,0:T(8,128)(2,1)} %get-tuple-element.48), channel_id=1, source_target_pairs={{0,128},{32,160},{64,192},{96,224},{128,0},{160,32},{192,64},{224,... | collective-permute-start | bytes 2457608 | tf_op jit(solution)/shard_map/ppermute | solution.py:335
  128.1 45.6 %collective-permute-start.10 = (bf16[320,1280]{1,0:T(8,128)(2,1)}, bf16[320,1280]{1,0:T(8,128)(2,1)}, u32[]{:S(2)}, u32[]{:S(2)}) collective-permute-start(bf16[320,1280]{1,0:T(8,128)(2,1)} %get-tuple-element.47), channel_id=1, source_target_pairs={{0,192},{32,224},{64,0},{96,32},{128,64},{160,96},{192,128},{224,1... | collective-permute-start | bytes 2457608 | tf_op jit(solution)/shard_map/ppermute | solution.py:335
  132.4 1.7 copy-start.5
  135.4 51.4 %collective-permute-start.4 = (bf16[4,160,1280]{2,1,0:T(8,128)(2,1)}, bf16[4,160,1280]{2,1,0:T(8,128)(2,1)}, u32[]{:S(2)}, u32[]{:S(2)}) collective-permute-start(bf16[4,160,1280]{2,1,0:T(8,128)(2,1)} %dynamic-slice_bitcast_fusion), channel_id=1, source_target_pairs={{0,32},{32,0},{64,96},{96,64},{128,160},{160,128},{192,224},{224,1... | collective-permute-start | bytes 4915208 | tf_op jit(solution)/shard_map/ppermute | solution.py:342
  150.4 18.6 %all-to-all-start.4 = ((f32[16,24,128]{2,1,0:T(8,128)}), f32[16,24,128]{2,1,0:T(8,128)S(1)}, u32[]{:S(2)}, u32[]{:S(2)}) async-start(f32[16,24,128]{2,1,0:T(8,128)} %bitcast.123), calls=%async_computation.4 | async-start | bytes 393216 | tf_op jit(solution)/shard_map/all_to_all | solution.py:510
  169.7 11.8 %all-to-all-start.5 = ((f32[16,24,128]{2,1,0:T(8,128)}), f32[16,24,128]{2,1,0:T(8,128)S(1)}, u32[]{:S(2)}, u32[]{:S(2)}) async-start(f32[16,24,128]{2,1,0:T(8,128)} %broadcast_in_dim.8), calls=%async_computation.5 | async-start | bytes 393216 | tf_op jit(solution)/shard_map/all_to_all | solution.py:32
  176.0 1.2 copy-start.4
  178.0 25.1 %collective-permute-start.11 = (bf16[160,1280]{1,0:T(8,128)(2,1)}, bf16[160,1280]{1,0:T(8,128)(2,1)}, u32[]{:S(2)}, u32[]{:S(2)}) collective-permute-start(bf16[160,1280]{1,0:T(8,128)(2,1)} %fusion.55), channel_id=1, source_target_pairs={{0,32},{32,0},{64,96},{96,64},{128,160},{160,128},{192,224},{224,1... | collective-permute-start | bytes 1228808 | tf_op jit(solution)/shard_map/ppermute | solution.py:342
  182.2 21.0 %all-to-all-start.6 = ((f32[16,24,128]{2,1,0:T(8,128)}), f32[16,24,128]{2,1,0:T(8,128)S(1)}, u32[]{:S(2)}, u32[]{:S(2)}) async-start(f32[16,24,128]{2,1,0:T(8,128)} %broadcast_in_dim.9), calls=%async_computation.6 | async-start | bytes 393216 | tf_op jit(solution)/shard_map/all_to_all | solution.py:32
  190.3 21.1 %collective-permute-start.5 = (bf16[160,1280]{1,0:T(8,128)(2,1)}, bf16[160,1280]{1,0:T(8,128)(2,1)}, u32[]{:S(2)}, u32[]{:S(2)}) collective-permute-start(bf16[160,1280]{1,0:T(8,128)(2,1)} %get-tuple-element.53), channel_id=1, source_target_pairs={{0,64},{32,96},{64,128},{96,160},{128,192},{160,224},{192,0},{224,... | collective-permute-start | bytes 1228808 | tf_op jit(solution)/shard_map/ppermute | solution.py:335
  190.4 21.1 %collective-permute-start.6 = (bf16[160,1280]{1,0:T(8,128)(2,1)}, bf16[160,1280]{1,0:T(8,128)(2,1)}, u32[]{:S(2)}, u32[]{:S(2)}) collective-permute-start(bf16[160,1280]{1,0:T(8,128)(2,1)} %get-tuple-element.52), channel_id=1, source_target_pairs={{0,128},{32,160},{64,192},{96,224},{128,0},{160,32},{192,64},{224,... | collective-permute-start | bytes 1228808 | tf_op jit(solution)/shard_map/ppermute | solution.py:335
  192.1 19.6 %collective-permute-start.7 = (bf16[160,1280]{1,0:T(8,128)(2,1)}, bf16[160,1280]{1,0:T(8,128)(2,1)}, u32[]{:S(2)}, u32[]{:S(2)}) collective-permute-start(bf16[160,1280]{1,0:T(8,128)(2,1)} %get-tuple-element.51), channel_id=1, source_target_pairs={{0,192},{32,224},{64,0},{96,32},{128,64},{160,96},{192,128},{224,1... | collective-permute-start | bytes 1228808 | tf_op jit(solution)/shard_map/ppermute | solution.py:335
  193.3 10.6 %copy-start.14 = (bf16[1280,32]{0,1:T(8,128)(2,1)S(1)}, bf16[1280,32]{0,1:T(8,128)(2,1)}, u32[]{:S(2)}) copy-start(bf16[1280,32]{0,1:T(8,128)(2,1)} %param.9) | copy-start | bytes 245764
  (2 other events, 1.6 us)

commit v3 on v2

--- a/solution.py
+++ b/solution.py
@@ -145,13 +145,13 @@
 
 def forward_kernel(images, *refs):
     inputs, outputs, held = refs[:3], refs[3:10], refs[10:]
-    tok, gain, keys, send, slots, normed, inverse, logs, disp, comb, mean, squares = held[:12]
-    in_sems, small_sems, exit_sems, out_sems = held[12:]
+    tok, flat, keys, send, slots, normed, inverse, logs, disp, comb, mean, squares, gain = held[:13]
+    in_sems, small_sems, exit_sems, out_sems = held[13:]
     count, features = tok.shape[1:]
     slot_count = keys.shape[0]
     tokens_in = [inputs[0].at[i] for i in range(images)]
     arrivals = started(copies_of(tokens_in, [tok.at[i] for i in range(images)], in_sems))
-    small_in = started(copies_of(inputs[1:], [gain, keys], small_sems))
+    small_in = started(copies_of(inputs[1:], [flat, keys], small_sems))
     exits = copies_of(
         [normed.at[i] for i in range(images)], [outputs[2].at[i] for i in range(images)], exit_sems
     )
@@ -180,6 +180,7 @@
     results[2].start()
     for copy in small_in:
         copy.wait()
+    gain[...] = flat[...].reshape(1, features)
     for i in range(images):
 
         def norm(rows):
@@ -327,6 +328,71 @@
     return [(i, (i + 2 * step) % size) for i in range(size)]
 
 
+def rotated_sum_kernel(where, far_part, far_other, *refs):
+    chips = far_other.shape[0]
+    outs, (part, other, sems) = refs[:chips], refs[chips:]
+    order = [lax.rem(where[0] + k, chips) for k in range(chips)]
+    copies = copies_of(
+        [far_part.at[at, where[1]] for at in order] + [far_other.at[at] for at in order],
+        [part.at[k] for k in range(chips)] + [other.at[k] for k in range(chips)],
+        sems,
+    )
+    started(copies)
+    for k in range(chips):
+        copies[k].wait()
+        copies[chips + k].wait()
+        outs[k][...] = added([part[k], other[k]]).astype(jnp.bfloat16)
+
+
+def rotated_sum(part, other):
+    chips, _, rows, cols = part.shape
+    index = lax.axis_index("dp")
+    where = jnp.stack([index // 2, index % 2]).astype(jnp.int32)
+    return call(
+        rotated_sum_kernel,
+        [((rows, cols), jnp.bfloat16, pl.BlockSpec(memory_space=pltpu.VMEM))] * chips,
+        [pl.BlockSpec(memory_space=pltpu.SMEM)] + [pl.BlockSpec(memory_space=pl.ANY)] * 2,
+        (where, part, other),
+        scratch=[pltpu.VMEM((chips, rows, cols), jnp.bfloat16)] * 2
+        + [pltpu.SemaphoreType.DMA((2 * chips,))],
+        flops=100 * rows * cols * chips,
+        moved=6 * rows * cols * chips,
+    )
+
+
+def split_sum_kernel(where, far_part, *refs):
+    arrived, (kept, sent, held, sems) = refs[:-4], refs[-4:]
+    chips = len(arrived) + 1
+    rows = kept.shape[0]
+    sources = [far_part.at[where[0]]] + list(arrived)
+    copies = started(copies_of(sources, [held.at[k] for k in range(chips)], sems))
+    for copy in copies:
+        copy.wait()
+
+    def total(low):
+        at = pl.ds(pl.multiple_of(low * rows, CHUNK), rows)
+        return added([held[k, at, :] for k in range(chips)])
+
+    kept[...] = total(where[1])
+    sent[...] = total(1 - where[1]).astype(jnp.bfloat16)
+
+
+def split_sum(part, arrived):
+    chips, rows, cols = part.shape
+    index = lax.axis_index("dp")
+    where = jnp.stack([index // 2, index % 2]).astype(jnp.int32)
+    local_ref = pl.BlockSpec(memory_space=pltpu.VMEM)
+    return call(
+        split_sum_kernel,
+        [((rows // 2, cols), jnp.float32, local_ref), ((rows // 2, cols), jnp.bfloat16, local_ref)],
+        [pl.BlockSpec(memory_space=pltpu.SMEM)] + [pl.BlockSpec(memory_space=pl.ANY)] * chips,
+        (where, part, *arrived),
+        scratch=[pltpu.VMEM((chips, rows, cols), jnp.bfloat16), pltpu.SemaphoreType.DMA((chips,))],
+        flops=100 * rows * cols * chips,
+        moved=2 * rows * cols * chips,
+    )
+
+
 def to_other_chips(pieces):
     size = lax.axis_size("dp")
     chips = size // 2
@@ -335,7 +401,7 @@
         lax.ppermute(piece_of(pieces, (at + step) % chips), "dp", chip_pairs(step, size))
         for step in range(1, chips)
     ]
-    return [piece_of(pieces, at)] + arrived
+    return arrived
 
 
 def to_neighbour(value):
@@ -383,10 +449,11 @@
         lambda *refs: forward_kernel(images, *refs),
         [(shape, kind, far_ref) for shape, kind in kept],
         [far_ref] * 3,
-        (tokens, gain, keys),
-        scratch=[stacked, pltpu.VMEM((1, features), f32), pltpu.VMEM((slot_count, features), bf16)]
+        (tokens, norm_gain, keys),
+        scratch=[stacked, pltpu.VMEM((features,), f32), pltpu.VMEM((slot_count, features), bf16)]
         + [pltpu.VMEM(shape, kind) for shape, kind in kept]
         + [pltpu.VMEM((images, count, LANES), f32)] * 2
+        + [pltpu.VMEM((1, features), f32)]
         + [pltpu.SemaphoreType.DMA((n,)) for n in (images, 2, images, 6)],
         flops=20 * small,
         moved=4 * images * count * features,
@@ -464,7 +531,6 @@
     grad_back = sent(to_send)
     first_sent = after(piece_of(first_part, 1 - low, 1), sums_in)
     first_other = to_neighbour(first_sent)
-    first_own = piece_of(first_part, low, 1)
 
     (combine_part,) = call(
         lambda *refs: combine_kernel(images, *refs),
@@ -511,17 +577,16 @@
     mine = jnp.sum(mine, axis=0)
     mine_two = from_everyone(mine, ("dp", "tensor"))
     first_other = after(first_other, mine)
-    first_half = added([first_own, first_other]).astype(bf16)
-    first_pieces = to_other_chips(first_half)
-    second_pieces = after(second_pieces, mine)
-    second_total = added(second_pieces).reshape(2, -1, features)
-    second_other = to_neighbour(piece_of(second_total, 1 - low).astype(bf16))
+    first_pieces = list(rotated_sum(first_part, first_other))
+    size = lax.axis_size("dp")
+    first_pieces = first_pieces[:1] + [
+        lax.ppermute(first_pieces[k], "dp", chip_pairs(k, size)) for k in range(1, chips)
+    ]
+    second_pieces = after(second_pieces, sums)
+    second_kept, second_sent = split_sum(second_part, second_pieces)
+    second_other = to_neighbour(second_sent)
     mine = jnp.sum(mine_two, axis=0)
     total = from_everyone(mine, "expert").reshape(-1, LANES)
-    first_pieces = after(first_pieces, mine)
-    grad_first = added(first_pieces).astype(bf16)
-    second_other = after(second_other, mine)
-    grad_second = added([piece_of(second_total, low), second_other]).astype(bf16)
     blocks = features // LANES
     keys_sum = total[: slot_count * blocks].reshape(blocks, slot_count, LANES)
     keys_sum = keys_sum.transpose(1, 0, 2).reshape(slot_count, features)
@@ -547,6 +612,10 @@
         flops=20 * small,
         moved=6 * images * count * features,
     )
+    first_pieces = after(first_pieces, grad_tokens)
+    grad_first = added(first_pieces).astype(bf16)
+    second_other = after(second_other, grad_tokens)
+    grad_second = added([second_kept, second_other]).astype(bf16)
     return (
         grad_tokens,
         gain_sum / norm_gain,

time: 216 us -> 215 us (level)
  blocking collectives: 0 us -> 18.6 us
  waiting for transfers between devices: 56.8 us -> 46.3 us
  starting transfers between devices: 62.6 us -> 54.4 us
  Pallas kernels: 46.4 us -> 54.2 us
  local copies, waits for them, and re-layouts: 15.2 us -> 10.1 us
  other arithmetic: 8.88 us -> 4.94 us
    all_to_all x0 -> x1, blocking collectives: none -> 18.6 us  [local(): lax.all_to_all(sums.reshape(group, ROWS, LANES), 'expert', 0, 0, tiled=True)]
    all_to_all x1 -> x0, waiting for transfers between devices: 10.2 us -> none  [local(): lax.all_to_all(sums.reshape(group, ROWS, LANES), 'expert', 0, 0, tiled=True)]
    all_to_all x1 -> x0, starting transfers between devices: 8.36 us -> none  [local(): lax.all_to_all(sums.reshape(group, ROWS, LANES), 'expert', 0, 0, tiled=True)]
    pallas_call x9 -> x11, Pallas kernels: 46.4 us -> 54.2 us  [call(): pl.pallas_call(kernel, out_shape=[jax.ShapeDtypeStruct(s, d) for s, d, _...]
    ppermute x6 -> x3, waiting for transfers between devices: 6.58 us -> 0.01 us  [to_other_chips(): lax.ppermute(piece_of(pieces, (at + step) % chips), 'dp', chip_pairs(step...]
    ppermute x0 -> x3, waiting for transfers between devices: none -> 6.57 us  [local(): lax.ppermute(first_pieces[k], 'dp', chip_pairs(k, size))]
    ppermute x0 -> x3, starting transfers between devices: none -> 3.04 us  [local(): lax.ppermute(first_pieces[k], 'dp', chip_pairs(k, size))]
    ppermute x6 -> x3, starting transfers between devices: 7.74 us -> 4.83 us  [to_other_chips(): lax.ppermute(piece_of(pieces, (at + step) % chips), 'dp', chip_pairs(step...]
  transfers between devices with their start and end apart: 19 -> 18, of which waited for: 8 -> 7; matrix products, arithmetic and copies ran while one was open for 18% -> 15% of each run, Pallas kernels for 16% -> 20%
where the time goes in v3:
time: 215 us; the launch traced here: 214 us
  starting transfers between devices  54.4 us (25%)
  Pallas kernels  54.2 us (25%)
  waiting for transfers between devices  46.3 us (22%)
  matrix products  24.2 us (11%)
  blocking collectives  18.6 us (9%)
  local copies, waits for them, and re-layouts  10.1 us (5%)
  other arithmetic  4.94 us (2%)
    pallas_call x11, Pallas kernels, call(): pl.pallas_call(kernel, out_shape=[jax.ShapeDtypeStruct(s, d) for s, d, _...  54.2 us
    all_to_all x4, starting transfers between devices, sent(): lax.all_to_all(shaped, 'expert', 0, 0, tiled=True).reshape(2 * rows, half)  26 us
    dot_general x10, matrix products, dot(): lax.dot_general(left, right, (dims, ((), ())), preferred_element_type=jnp...  24.2 us
    all_to_all x4, waiting for transfers between devices, sent(): lax.all_to_all(shaped, 'expert', 0, 0, tiled=True).reshape(2 * rows, half)  21.3 us
    all_to_all x1, blocking collectives, local(): lax.all_to_all(sums.reshape(group, ROWS, LANES), 'expert', 0, 0, tiled=True)  18.6 us
    ppermute x4, waiting for transfers between devices, swapped(): return lax.ppermute(value, 'tensor', [(0, 1), (1, 0)])  16.6 us
    ppermute x4, starting transfers between devices, swapped(): return lax.ppermute(value, 'tensor', [(0, 1), (1, 0)])  9.15 us
    all_to_all x2, starting transfers between devices, from_everyone(): lax.all_to_all(jnp.broadcast_to(shard[None], (devices, *shard.shape)), ax...  8.67 us
  transfers between devices with their start and end apart: 18, of which 7 were waited for; matrix products, arithmetic and copies ran while one was open for 15% of the time, Pallas kernels for 20%

profile of v3, /device:TPU:1, one launch (start us, length us, event | category | flops | bytes accessed | tf_op | source)
XLA Modules:
  0.0 213.7 jit_solution(14419784726253746644)
XLA Ops:
  0.6 11.7 %shard_map.101 = (bf16[384,640]{1,0:T(8,128)(2,1)}, bf16[192,1280]{1,0:T(8,128)(2,1)}, bf16[6,256,1280]{2,1,0:T(8,128)(2,1)}, f32[6,256,128]{2,1,0:T(8,128)}, f3...) custom-call(bf16[6,256,1280]{2,1,0:T(8,128)(2,1)} %refs_0_.2, f32[1280]{0:T(1024)} %refs_1_.2, ...), custom_call_target="tpu_custom_call" | custom-call | flops 2516582400 | bytes 7864320 | tf_op jit(solution)/shard_map/pallas_call | solution.py:43
  12.3 10.0 %all-to-all-start.1 = ((bf16[16,24,640]{2,1,0:T(8,128)(2,1)}), bf16[16,24,640]{2,1,0:T(8,128)(2,1)}, u32[]{:S(2)}, u32[]{:S(2)}) async-start(bf16[16,24,640]{2,1,0:T(8,128)(2,1)} %bitcast.98), calls=%async_computation.1 | async-start | bytes 983040 | tf_op jit(solution)/shard_map/all_to_all | solution.py:434
  22.3 5.7 %shard_map.102 = bf16[384,640]{1,0:T(8,128)(2,1)} custom-call(bf16[6,256,1280]{2,1,0:T(8,128)(2,1)} %cot.1, f32[6,32,256]{2,1,0:T(8,128)} %get-tuple-element.33.refs_1_.refs_2_), custom_call_target="tpu_custom_call" | custom-call | flops 1258291200 | bytes 3932160 | tf_op jit(solution)/shard_map/pallas_call | solution.py:43
  28.0 11.0 %all-to-all-done.1 = bf16[16,24,640]{2,1,0:T(8,128)(2,1)} async-done(((bf16[16,24,640]{2,1,0:T(8,128)(2,1)}), bf16[16,24,640]{2,1,0:T(8,128)(2,1)}, u32[]{:S(2)}, u32[]{:S(2)}) %all-to-all-start.1) | async-done | bytes 491552 | tf_op jit(solution)/shard_map/all_to_all | solution.py:434
  38.9 4.1 %all-to-all-start = ((bf16[16,24,640]{2,1,0:T(8,128)(2,1)}), bf16[16,24,640]{2,1,0:T(8,128)(2,1)}, u32[]{:S(2)}, u32[]{:S(2)}) async-start(bf16[16,24,640]{2,1,0:T(8,128)(2,1)} %bitcast.97), calls=%async_computation | async-start | bytes 983040 | tf_op jit(solution)/shard_map/all_to_all | solution.py:434
  43.1 2.3 %shard_map.104 = bf16[192,1280]{1,0:T(8,128)(2,1)} custom-call(bf16[384,640]{1,0:T(8,128)(2,1)} %bitcast.5.refs_0_), custom_call_target="tpu_custom_call" | custom-call | flops 503316480 | bytes 983040 | tf_op jit(solution)/shard_map/pallas_call | solution.py:43
  45.4 2.9 %collective-permute-start.1 = (bf16[192,1280]{1,0:T(8,128)(2,1)}, bf16[192,1280]{1,0:T(8,128)(2,1)}, u32[]{:S(2)}, u32[]{:S(2)}) collective-permute-start(bf16[192,1280]{1,0:T(8,128)(2,1)} %shard_map.104), channel_id=1, source_target_pairs={{0,1},{1,0},{2,3},{3,2},{4,5},{5,4},{6,7},{7,6},{8,9},{9,8},{10,11... | collective-permute-start | bytes 1474568 | tf_op jit(solution)/shard_map/ppermute | solution.py:38
  48.3 10.3 %all-to-all-done = bf16[16,24,640]{2,1,0:T(8,128)(2,1)} async-done(((bf16[16,24,640]{2,1,0:T(8,128)(2,1)}), bf16[16,24,640]{2,1,0:T(8,128)(2,1)}, u32[]{:S(2)}, u32[]{:S(2)}) %all-to-all-start) | async-done | bytes 491552 | tf_op jit(solution)/shard_map/all_to_all | solution.py:434
  58.6 2.3 %shard_map.103 = bf16[192,1280]{1,0:T(8,128)(2,1)} custom-call(bf16[384,640]{1,0:T(8,128)(2,1)} %bitcast.2.refs_0_), custom_call_target="tpu_custom_call" | custom-call | flops 503316480 | bytes 983040 | tf_op jit(solution)/shard_map/pallas_call | solution.py:43
  60.9 2.9 %collective-permute-start = (bf16[192,1280]{1,0:T(8,128)(2,1)}, bf16[192,1280]{1,0:T(8,128)(2,1)}, u32[]{:S(2)}, u32[]{:S(2)}) collective-permute-start(bf16[192,1280]{1,0:T(8,128)(2,1)} %shard_map.103), channel_id=1, source_target_pairs={{0,1},{1,0},{2,3},{3,2},{4,5},{5,4},{6,7},{7,6},{8,9},{9,8},{10,11... | collective-permute-start | bytes 1474568 | tf_op jit(solution)/shard_map/ppermute | solution.py:38
  65.8 3.1 %multiply_convert_fusion = (bf16[192,1280]{1,0:T(8,128)(2,1)S(1)}, f32[192,1280]{1,0:T(8,128)}) fusion(bf16[192,1280]{1,0:T(8,128)(2,1)} %collective-permute-done.1, bf16[1,1280,1280]{2,1,0:T(8,128)(2,1)S(1)} %copy-done), kind=kOutput, calls=%fused_computation.51 | convolution fusion | flops 631357440 | bytes 5242880 | tf_op jit(solution)/shard_map/dot_general | solution.py:22
  70.8 3.2 %fusion.28 = bf16[192,1280]{1,0:T(8,128)(2,1)} fusion(f32[192,1280]{1,0:T(8,128)S(1)} %get-tuple-element.61, bf16[192,1280]{1,0:T(8,128)(2,1)} %shard_map.103, bf16[1,1280,1280]{2,1,0:T(8,128)(2,1)S(1)} %copy-done.3), kind=kOutput, calls=%fused_computation.31 | convolution fusion | flops 634060800 | bytes 5242880 | tf_op jit(solution)/shard_map/dot_general | solution.py:22
  74.1 11.4 %collective-permute-done.3.refs_1_ = bf16[192,1280]{1,0:T(8,128)(2,1)S(1)} collective-permute-done((bf16[192,1280]{1,0:T(8,128)(2,1)S(1)}, bf16[192,1280]{1,0:T(8,128)(2,1)S(1)}, u32[]{:S(2)}, u32[]{:S(2)}) %collective-permute-start.3) | collective-permute-done | bytes 491552 | tf_op jit(solution)/shard_map/ppermute | solution.py:38
  86.9 4.1 %all-to-all-start.3 = ((bf16[16,24,640]{2,1,0:T(8,128)(2,1)}), bf16[16,24,640]{2,1,0:T(8,128)(2,1)}, u32[]{:S(2)}, u32[]{:S(2)}) async-start(bf16[16,24,640]{2,1,0:T(8,128)(2,1)} %bitcast.88), calls=%async_computation.3 | async-start | bytes 983040 | tf_op jit(solution)/shard_map/all_to_all | solution.py:434
  91.0 3.7 %fusion.35 = bf16[192,1280]{1,0:T(8,128)(2,1)S(1)} fusion(f32[192,1280]{1,0:T(8,128)} %get-tuple-element.63, bf16[192,1280]{1,0:T(8,128)(2,1)} %collective-permute-done, bf16[1,1280,1280]{2,1,0:T(8,128)(2,1)} %param.11), kind=kOutput, calls=%fused_computation.38 | convolution fusion | flops 634060800 | bytes 5242880 | tf_op jit(solution)/shard_map/dot_general | solution.py:22
  96.0 3.0 %collective-permute-start.2 = (bf16[192,1280]{1,0:T(8,128)(2,1)S(1)}, bf16[192,1280]{1,0:T(8,128)(2,1)S(1)}, u32[]{:S(2)}, u32[]{:S(2)}) collective-permute-start(bf16[192,1280]{1,0:T(8,128)(2,1)S(1)} %fusion.19), channel_id=1, source_target_pairs={{0,1},{1,0},{2,3},{3,2},{4,5},{5,4},{6,7},{7,6},{8,9},{9,8},{10,11... | collective-permute-start | bytes 1474568 | tf_op jit(solution)/shard_map/ppermute | solution.py:38
  100.2 4.8 %convolution_convert_fusion.1 = bf16[1280,1280]{1,0:T(8,128)(2,1)} fusion(bf16[192,1280]{1,0:T(8,128)(2,1)} %collective-permute-done.1, bf16[192,1280]{1,0:T(8,128)(2,1)} %shard_map.104, bf16[192,1280]{1,0:T(8,128)(2,1)S(1)} %fusion.35, bf16[192,1280]{1,0:T(8,128)(2,1)S(1)} %copy-done.6), kind=kOutput, calls=%fused_computation.1 | convolution fusion | flops 1263861760 | bytes 5242880 | tf_op jit(solution)/shard_map/dot_general | solution.py:22
  105.0 5.2 %collective-permute-done.2.refs_1_ = bf16[192,1280]{1,0:T(8,128)(2,1)S(1)} collective-permute-done((bf16[192,1280]{1,0:T(8,128)(2,1)S(1)}, bf16[192,1280]{1,0:T(8,128)(2,1)S(1)}, u32[]{:S(2)}, u32[]{:S(2)}) %collective-permute-start.2) | collective-permute-done | bytes 491552 | tf_op jit(solution)/shard_map/ppermute | solution.py:38
  111.6 7.8 %all-to-all-start.2 = ((bf16[16,24,640]{2,1,0:T(8,128)(2,1)}), bf16[16,24,640]{2,1,0:T(8,128)(2,1)}, u32[]{:S(2)}, u32[]{:S(2)}) async-start(bf16[16,24,640]{2,1,0:T(8,128)(2,1)} %bitcast.87), calls=%async_computation.2 | async-start | bytes 983040 | tf_op jit(solution)/shard_map/all_to_all | solution.py:434
  119.4 2.7 %dynamic-slice_bitcast_fusion = bf16[4,160,1280]{2,1,0:T(8,128)(2,1)} fusion(bf16[4,2,160,1280]{3,2,1,0:T(8,128)(2,1)} %bitcast.91, s32[]{:T(128)S(6)} %select_n.45), kind=kLoop, calls=%fused_computation.20 | loop fusion | bytes 3276804 | tf_op jit(solution)/shard_map/jit(dynamic_index_in_dim)/squeeze | solution.py:324
  123.4 3.4 %convolution_convert_fusion = bf16[1280,1280]{1,0:T(8,128)(2,1)S(1)} fusion(bf16[192,1280]{1,0:T(8,128)(2,1)} %collective-permute-done, bf16[192,1280]{1,0:T(8,128)(2,1)} %shard_map.103, bf16[192,1280]{1,0:T(8,128)(2,1)} %copy-done.7, bf16[192,1280]{1,0:T(8,128)(2,1)} %copy-done.5), kind=kOutput, calls=%fused_computation | convolution fusion | flops 1263861760 | bytes 5242880 | tf_op jit(solution)/shard_map/dot_general | solution.py:22
  131.2 2.4 %collective-permute-start.9 = (bf16[320,1280]{1,0:T(8,128)(2,1)}, bf16[320,1280]{1,0:T(8,128)(2,1)}, u32[]{:S(2)}, u32[]{:S(2)}) collective-permute-start(bf16[320,1280]{1,0:T(8,128)(2,1)} %get-tuple-element.58), channel_id=1, source_target_pairs={{0,128},{32,160},{64,192},{96,224},{128,0},{160,32},{192,64},{224,... | collective-permute-start | bytes 2457608 | tf_op jit(solution)/shard_map/ppermute | solution.py:401
  135.4 6.1 %shard_map.107.refs_5_ = f32[6,32,256]{2,1,0:T(8,128)} custom-call(bf16[384,640]{1,0:T(8,128)(2,1)} %bitcast.10.refs_0_, bf16[6,256,1280]{2,1,0:T(8,128)(2,1)} %cot.1, f32[6,32,256]{2,1,0:T(8,128)} %get-tuple-element.33.refs_1_.refs_2_), custom_call_target="tpu_custom_call" | custom-call | flops 1258291200 | bytes 3932160 | tf_op jit(solution)/shard_map/pallas_call | solution.py:43
  141.5 7.6 %shard_map.108 = (bf16[192,1280]{1,0:T(8,128)(2,1)}, bf16[6,80,256]{2,1,0:T(8,128)(2,1)}, f32[384,128]{1,0:T(8,128)}) custom-call(bf16[384,640]{1,0:T(8,128)(2,1)} %bitcast.8.refs_0_, bf16[192,1280]{1,0:T(8,128)(2,1)} %get-tuple-element.35.refs_1_, bf16[6,256,1280]{2,1,0:T(8,128)(2,1)} %get-tuple-element.31.refs_2_.normed, ...), custom_call_target="tpu_custom_call" | custom-call | flops 1887436800 | bytes 3932160 | tf_op jit(solution)/shard_map/pallas_call | solution.py:43
  149.0 18.6 %all_to_all.35 = f32[16,24,128]{2,1,0:T(8,128)S(1)} all-to-all(f32[16,24,128]{2,1,0:T(8,128)} %bitcast.102), channel_id=1, replica_groups=mesh['dp'=8,'expert'=16,'tensor'=2] {'expert'}, dimensions={0} | all-to-all | bytes 393216 | tf_op jit(solution)/shard_map/all_to_all | solution.py:576
  168.3 4.0 %all-to-all-start.5 = ((f32[16,24,128]{2,1,0:T(8,128)}), f32[16,24,128]{2,1,0:T(8,128)S(1)}, u32[]{:S(2)}, u32[]{:S(2)}) async-start(f32[16,24,128]{2,1,0:T(8,128)} %broadcast_in_dim.8), calls=%async_computation.5 | async-start | bytes 393216 | tf_op jit(solution)/shard_map/all_to_all | solution.py:32
  173.0 3.8 %shard_map.111 = (f32[160,1280]{1,0:T(8,128)}, bf16[160,1280]{1,0:T(8,128)(2,1)}) custom-call(s32[2]{0:T(128)} %pad_add_fusion.where, bf16[4,320,1280]{2,1,0:T(8,128)(2,1)} %bitcast.90, bf16[320,1280]{1,0:T(8,128)(2,1)} %collective-permute-done.8.refs_0_, bf16[320,1280]{1,0:T(8,128)(2,1)} %collective-permute-done.9.refs_1_, ...), custom_call_target="tpu_custom_call" | custom-call | flops 163840000 | bytes 3276800 | tf_op jit(solution)/shard_map/pallas_call | solution.py:43
  180.8 4.7 %all-to-all-start.6 = ((f32[16,24,128]{2,1,0:T(8,128)}), f32[16,24,128]{2,1,0:T(8,128)S(1)}, u32[]{:S(2)}, u32[]{:S(2)}) async-start(f32[16,24,128]{2,1,0:T(8,128)} %broadcast_in_dim.9), calls=%async_computation.6 | async-start | bytes 393216 | tf_op jit(solution)/shard_map/all_to_all | solution.py:32
  185.4 3.8 %shard_map.110 = (bf16[160,1280]{1,0:T(8,128)(2,1)}, bf16[160,1280]{1,0:T(8,128)(2,1)}, bf16[160,1280]{1,0:T(8,128)(2,1)}, bf16[160,1280]{1,0:T(8,128)(2,1)}) custom-call(s32[2]{0:T(128)} %pad_add_fusion.where, bf16[4,2,160,1280]{3,2,1,0:T(8,128)(2,1)} %bitcast.92, bf16[4,160,1280]{2,1,0:T(8,128)(2,1)} %collective-permute-done.4.far_other), custom_call_target="tpu_custom_call" | custom-call | flops 81920000 | bytes 4915200 | tf_op jit(solution)/shard_map/pallas_call | solution.py:43
  192.3 9.8 %shard_map.109 = bf16[6,256,1280]{2,1,0:T(8,128)(2,1)} custom-call(bf16[6,256,1280]{2,1,0:T(8,128)(2,1)} %get-tuple-element.31.refs_2_.normed, bf16[6,256,1280]{2,1,0:T(8,128)(2,1)} %cot.1, f32[6,256,128]{2,1,0:T(8,128)} %get-tuple-element.32.inverse, bf16[6,80,256]{2,1,0:T(8,128)(2,1)} %get-tuple-element.38.pair, ...), custom_call_target="tpu_custom_call" | custom-call | flops 2516582400 | bytes 11796480 | tf_op jit(solution)/shard_map/pallas_call | solution.py:43
  204.2 6.2 %collective-permute-done.5 = bf16[160,1280]{1,0:T(8,128)(2,1)} collective-permute-done((bf16[160,1280]{1,0:T(8,128)(2,1)}, bf16[160,1280]{1,0:T(8,128)(2,1)}, u32[]{:S(2)}, u32[]{:S(2)}) %collective-permute-start.5) | collective-permute-done | bytes 409632 | tf_op jit(solution)/shard_map/ppermute | solution.py:583
  210.8 2.9 %fusion.52 = (bf16[1,160,1280]{2,1,0:T(8,128)(2,1)}, bf16[1,1280,160]{1,2,0:T(8,128)(2,1)}) fusion(bf16[160,1280]{1,0:T(8,128)(2,1)} %collective-permute-done.7, bf16[160,1280]{1,0:T(8,128)(2,1)} %collective-permute-done.6, bf16[160,1280]{1,0:T(8,128)(2,1)} %collective-permute-done.5, bf16[160,1280]{1,0:T(8,128)(2,1)} %get-tuple-element.47, ...), kind=kLoop, calls=%fused_computation.58 | loop fusion | flops 2252800 | bytes 3686400 | tf_op jit(solution)/shard_map/broadcast_in_dim | solution.py:623
  (59 shorter events, 27.3 us)
Async XLA Ops:
  0.6 63.2 %copy-start = (bf16[1,1280,1280]{2,1,0:T(8,128)(2,1)S(1)}, bf16[1,1280,1280]{2,1,0:T(8,128)(2,1)}, u32[]{:S(2)}) copy-start(bf16[1,1280,1280]{2,1,0:T(8,128)(2,1)} %param.10) | copy-start | bytes 9830404
  12.3 26.6 %all-to-all-start.1 = ((bf16[16,24,640]{2,1,0:T(8,128)(2,1)}), bf16[16,24,640]{2,1,0:T(8,128)(2,1)}, u32[]{:S(2)}, u32[]{:S(2)}) async-start(bf16[16,24,640]{2,1,0:T(8,128)(2,1)} %bitcast.98), calls=%async_computation.1 | async-start | bytes 983040 | tf_op jit(solution)/shard_map/all_to_all | solution.py:434
  38.9 19.7 %all-to-all-start = ((bf16[16,24,640]{2,1,0:T(8,128)(2,1)}), bf16[16,24,640]{2,1,0:T(8,128)(2,1)}, u32[]{:S(2)}, u32[]{:S(2)}) async-start(bf16[16,24,640]{2,1,0:T(8,128)(2,1)} %bitcast.97), calls=%async_computation | async-start | bytes 983040 | tf_op jit(solution)/shard_map/all_to_all | solution.py:434
  45.4 20.4 %collective-permute-start.1 = (bf16[192,1280]{1,0:T(8,128)(2,1)}, bf16[192,1280]{1,0:T(8,128)(2,1)}, u32[]{:S(2)}, u32[]{:S(2)}) collective-permute-start(bf16[192,1280]{1,0:T(8,128)(2,1)} %shard_map.104), channel_id=1, source_target_pairs={{0,1},{1,0},{2,3},{3,2},{4,5},{5,4},{6,7},{7,6},{8,9},{9,8},{10,11... | collective-permute-start | bytes 1474568 | tf_op jit(solution)/shard_map/ppermute | solution.py:38
  60.9 30.1 %collective-permute-start = (bf16[192,1280]{1,0:T(8,128)(2,1)}, bf16[192,1280]{1,0:T(8,128)(2,1)}, u32[]{:S(2)}, u32[]{:S(2)}) collective-permute-start(bf16[192,1280]{1,0:T(8,128)(2,1)} %shard_map.103), channel_id=1, source_target_pairs={{0,1},{1,0},{2,3},{3,2},{4,5},{5,4},{6,7},{7,6},{8,9},{9,8},{10,11... | collective-permute-start | bytes 1474568 | tf_op jit(solution)/shard_map/ppermute | solution.py:38
  65.7 4.2 %copy-start.5 = (bf16[192,1280]{1,0:T(8,128)(2,1)}, bf16[192,1280]{1,0:T(8,128)(2,1)S(1)}, u32[]{:S(2)}) copy-start(bf16[192,1280]{1,0:T(8,128)(2,1)S(1)} %get-tuple-element.60) | copy-start | bytes 1474564
  65.7 3.1 %copy-start.3 = (bf16[1,1280,1280]{2,1,0:T(8,128)(2,1)S(1)}, bf16[1,1280,1280]{2,1,0:T(8,128)(2,1)}, u32[]{:S(2)}) copy-start(bf16[1,1280,1280]{2,1,0:T(8,128)(2,1)} %param.11) | copy-start | bytes 9830404
  68.8 2.0 copy-start.7
  69.6 15.8 %collective-permute-start.3 = (bf16[192,1280]{1,0:T(8,128)(2,1)S(1)}, bf16[192,1280]{1,0:T(8,128)(2,1)S(1)}, u32[]{:S(2)}, u32[]{:S(2)}) collective-permute-start(bf16[192,1280]{1,0:T(8,128)(2,1)S(1)} %fusion.16), channel_id=1, source_target_pairs={{0,1},{1,0},{2,3},{3,2},{4,5},{5,4},{6,7},{7,6},{8,9},{9,8},{10,11... | collective-permute-start | bytes 1474568 | tf_op jit(solution)/shard_map/ppermute | solution.py:38
  86.1 0.8 copy-start.2
  86.9 24.7 %all-to-all-start.3 = ((bf16[16,24,640]{2,1,0:T(8,128)(2,1)}), bf16[16,24,640]{2,1,0:T(8,128)(2,1)}, u32[]{:S(2)}, u32[]{:S(2)}) async-start(bf16[16,24,640]{2,1,0:T(8,128)(2,1)} %bitcast.88), calls=%async_computation.3 | async-start | bytes 983040 | tf_op jit(solution)/shard_map/all_to_all | solution.py:434
  94.7 4.2 %copy-start.6 = (bf16[192,1280]{1,0:T(8,128)(2,1)S(1)}, bf16[192,1280]{1,0:T(8,128)(2,1)}, u32[]{:S(2)}) copy-start(bf16[192,1280]{1,0:T(8,128)(2,1)} %fusion.28) | copy-start | bytes 1474564
  96.0 14.2 %collective-permute-start.2 = (bf16[192,1280]{1,0:T(8,128)(2,1)S(1)}, bf16[192,1280]{1,0:T(8,128)(2,1)S(1)}, u32[]{:S(2)}, u32[]{:S(2)}) collective-permute-start(bf16[192,1280]{1,0:T(8,128)(2,1)S(1)} %fusion.19), channel_id=1, source_target_pairs={{0,1},{1,0},{2,3},{3,2},{4,5},{5,4},{6,7},{7,6},{8,9},{9,8},{10,11... | collective-permute-start | bytes 1474568 | tf_op jit(solution)/shard_map/ppermute | solution.py:38
  110.8 0.8 copy-start.1
  111.6 29.9 %all-to-all-start.2 = ((bf16[16,24,640]{2,1,0:T(8,128)(2,1)}), bf16[16,24,640]{2,1,0:T(8,128)(2,1)}, u32[]{:S(2)}, u32[]{:S(2)}) async-start(bf16[16,24,640]{2,1,0:T(8,128)(2,1)} %bitcast.87), calls=%async_computation.2 | async-start | bytes 983040 | tf_op jit(solution)/shard_map/all_to_all | solution.py:434
  122.1 63.3 %collective-permute-start.4 = (bf16[4,160,1280]{2,1,0:T(8,128)(2,1)}, bf16[4,160,1280]{2,1,0:T(8,128)(2,1)}, u32[]{:S(2)}, u32[]{:S(2)}) collective-permute-start(bf16[4,160,1280]{2,1,0:T(8,128)(2,1)} %dynamic-slice_bitcast_fusion), channel_id=1, source_target_pairs={{0,32},{32,0},{64,96},{96,64},{128,160},{160,128},{192,224},{224,1... | collective-permute-start | bytes 4915208 | tf_op jit(solution)/shard_map/ppermute | solution.py:408
  126.8 1.7 copy-start.4
  126.8 8.0 %copy-start.9 = (f32[1280]{0:T(1024)S(1)}, f32[1280]{0:T(1024)}, u32[]{:S(2)}) copy-start(f32[1280]{0:T(1024)} %refs_1_.2) | copy-start | bytes 15364
  129.9 43.0 %collective-permute-start.8 = (bf16[320,1280]{1,0:T(8,128)(2,1)}, bf16[320,1280]{1,0:T(8,128)(2,1)}, u32[]{:S(2)}, u32[]{:S(2)}) collective-permute-start(bf16[320,1280]{1,0:T(8,128)(2,1)} %get-tuple-element.59), channel_id=1, source_target_pairs={{0,64},{32,96},{64,128},{96,160},{128,192},{160,224},{192,0},{224,... | collective-permute-start | bytes 2457608 | tf_op jit(solution)/shard_map/ppermute | solution.py:401
  131.2 41.8 %collective-permute-start.9 = (bf16[320,1280]{1,0:T(8,128)(2,1)}, bf16[320,1280]{1,0:T(8,128)(2,1)}, u32[]{:S(2)}, u32[]{:S(2)}) collective-permute-start(bf16[320,1280]{1,0:T(8,128)(2,1)} %get-tuple-element.58), channel_id=1, source_target_pairs={{0,128},{32,160},{64,192},{96,224},{128,0},{160,32},{192,64},{224,... | collective-permute-start | bytes 2457608 | tf_op jit(solution)/shard_map/ppermute | solution.py:401
  133.6 39.4 %collective-permute-start.10 = (bf16[320,1280]{1,0:T(8,128)(2,1)}, bf16[320,1280]{1,0:T(8,128)(2,1)}, u32[]{:S(2)}, u32[]{:S(2)}) collective-permute-start(bf16[320,1280]{1,0:T(8,128)(2,1)} %get-tuple-element.57), channel_id=1, source_target_pairs={{0,192},{32,224},{64,0},{96,32},{128,64},{160,96},{192,128},{224,1... | collective-permute-start | bytes 2457608 | tf_op jit(solution)/shard_map/ppermute | solution.py:401
  168.3 11.8 %all-to-all-start.5 = ((f32[16,24,128]{2,1,0:T(8,128)}), f32[16,24,128]{2,1,0:T(8,128)S(1)}, u32[]{:S(2)}, u32[]{:S(2)}) async-start(f32[16,24,128]{2,1,0:T(8,128)} %broadcast_in_dim.8), calls=%async_computation.5 | async-start | bytes 393216 | tf_op jit(solution)/shard_map/all_to_all | solution.py:32
  176.8 25.3 %collective-permute-start.11 = (bf16[160,1280]{1,0:T(8,128)(2,1)}, bf16[160,1280]{1,0:T(8,128)(2,1)}, u32[]{:S(2)}, u32[]{:S(2)}) collective-permute-start(bf16[160,1280]{1,0:T(8,128)(2,1)} %get-tuple-element.55), channel_id=1, source_target_pairs={{0,32},{32,0},{64,96},{96,64},{128,160},{160,128},{192,224},{224,1... | collective-permute-start | bytes 1228808 | tf_op jit(solution)/shard_map/ppermute | solution.py:408
  180.8 21.4 %all-to-all-start.6 = ((f32[16,24,128]{2,1,0:T(8,128)}), f32[16,24,128]{2,1,0:T(8,128)S(1)}, u32[]{:S(2)}, u32[]{:S(2)}) async-start(f32[16,24,128]{2,1,0:T(8,128)} %broadcast_in_dim.9), calls=%async_computation.6 | async-start | bytes 393216 | tf_op jit(solution)/shard_map/all_to_all | solution.py:32
  189.2 21.2 %collective-permute-start.5 = (bf16[160,1280]{1,0:T(8,128)(2,1)}, bf16[160,1280]{1,0:T(8,128)(2,1)}, u32[]{:S(2)}, u32[]{:S(2)}) collective-permute-start(bf16[160,1280]{1,0:T(8,128)(2,1)} %get-tuple-element.44), channel_id=1, source_target_pairs={{0,64},{32,96},{64,128},{96,160},{128,192},{160,224},{192,0},{224,... | collective-permute-start | bytes 1228808 | tf_op jit(solution)/shard_map/ppermute | solution.py:583
  189.3 21.1 %collective-permute-start.6 = (bf16[160,1280]{1,0:T(8,128)(2,1)}, bf16[160,1280]{1,0:T(8,128)(2,1)}, u32[]{:S(2)}, u32[]{:S(2)}) collective-permute-start(bf16[160,1280]{1,0:T(8,128)(2,1)} %get-tuple-element.45), channel_id=1, source_target_pairs={{0,128},{32,160},{64,192},{96,224},{128,0},{160,32},{192,64},{224,... | collective-permute-start | bytes 1228808 | tf_op jit(solution)/shard_map/ppermute | solution.py:583
  191.1 19.6 %collective-permute-start.7 = (bf16[160,1280]{1,0:T(8,128)(2,1)}, bf16[160,1280]{1,0:T(8,128)(2,1)}, u32[]{:S(2)}, u32[]{:S(2)}) collective-permute-start(bf16[160,1280]{1,0:T(8,128)(2,1)} %get-tuple-element.46), channel_id=1, source_target_pairs={{0,192},{32,224},{64,0},{96,32},{128,64},{160,96},{192,128},{224,1... | collective-permute-start | bytes 1228808 | tf_op jit(solution)/shard_map/ppermute | solution.py:583
  192.3 10.6 %copy-start.8 = (bf16[1280,32]{0,1:T(8,128)(2,1)S(1)}, bf16[1280,32]{0,1:T(8,128)(2,1)}, u32[]{:S(2)}) copy-start(bf16[1280,32]{0,1:T(8,128)(2,1)} %param.9) | copy-start | bytes 245764

commit v4 on v3

--- a/solution.py
+++ b/solution.py
@@ -192,6 +192,7 @@
 
         over_chunks(count, norm)
         exits[i].start()
+    for i in range(images):
         logs[i] = dot(keys[...], normed[i], NT)
     results[3].start()
     for i in range(images):
@@ -237,9 +238,11 @@
         copy.wait()
     unpack_into(slots, back[...], images, True)
     count = comb.shape[1]
-    for i in range(images):
-        arrivals[i].wait()
-        grad = dot(slots[i * count : (i + 1) * count, :], cot[i], NT)
+    for copy in arrivals:
+        copy.wait()
+    grad_all = [dot(slots[i * count : (i + 1) * count, :], cot[i], NT) for i in range(images)]
+    for i in range(images):
+        grad = grad_all[i]
         weight = comb[i]
         out[i] = weight * (grad - jnp.sum(weight * grad, axis=0, keepdims=True))
 
@@ -261,17 +264,22 @@
     share = 1.0 / normed.shape[2]
     keys_share = jnp.sum(keys[...].astype(jnp.float32) * gain[...], axis=1, keepdims=True)
     place = lax.broadcasted_iota(jnp.int32, (16, tokens), 0)
-    for i in range(images):
-        arrivals[i].wait()
+    grad_all = []
+    for copy in arrivals:
+        copy.wait()
+    for i in range(images):
         mine = grads[i * count : (i + 1) * count, :]
-        grad = dot(mine, normed[i], NT)
+        grad_all.append(dot(mine, normed[i], NT))
+    updates = []
+    for i in range(images):
+        mine = grads[i * count : (i + 1) * count, :]
+        grad = grad_all[i]
         weight = disp[i]
         wide = weight * (grad - jnp.sum(weight * grad, axis=1, keepdims=True)) + part[i]
         high, rest = parts(wide, 2)
         pair[i, :count, :] = high
         pair[i, count : 2 * count, :] = rest
-        update = dot(pair[i, : 2 * count, :], normed[i], NN)
-        total[...] = update if i == 0 else total[...] + update
+        updates.append(jnp.concatenate([high, rest], axis=0))
         used = high.astype(jnp.float32) + rest.astype(jnp.float32)
         spread = weight.astype(jnp.bfloat16).astype(jnp.float32)
         mine_share = jnp.sum(mine.astype(jnp.float32) * gain[...], axis=1, keepdims=True)
@@ -281,6 +289,8 @@
         for k, row in enumerate(parts(first, 2) + parts(second, 2)):
             rows = jnp.where(place == k, row.astype(jnp.float32), rows)
         pair[i, 2 * count :, :] = rows.astype(jnp.bfloat16)
+    flat = normed[...].reshape(images * tokens, normed.shape[2])
+    total[...] = dot(jnp.concatenate(updates, axis=1), flat, NN)
     product = grads[...].astype(jnp.float32) * slots[...].astype(jnp.float32)
     moved = jnp.sum(product, axis=0, keepdims=True)
     blocks = moved.shape[1] // LANES

time: 215 us -> 212 us (0.986)
  Pallas kernels: 54.2 us -> 49 us
  starting transfers between devices: 54.4 us -> 57.8 us
    pallas_call x11, Pallas kernels: 54.2 us -> 49 us  [call(): pl.pallas_call(kernel, out_shape=[jax.ShapeDtypeStruct(s, d) for s, d, _...]
  transfers between devices with their start and end apart: 18 -> 18, of which waited for: 7 -> 6; matrix products, arithmetic and copies ran while one was open for 15% -> 16% of each run, Pallas kernels for 20% -> 19%
where the time goes in v4:
time: 212 us; the launch traced here: 210 us
  starting transfers between devices  57.8 us (27%)
  Pallas kernels  49 us (23%)
  waiting for transfers between devices  44.6 us (21%)
  matrix products  24.2 us (11%)
  blocking collectives  18.6 us (9%)
  local copies, waits for them, and re-layouts  10.1 us (5%)
  other arithmetic  4.94 us (2%)
    pallas_call x11, Pallas kernels, call(): pl.pallas_call(kernel, out_shape=[jax.ShapeDtypeStruct(s, d) for s, d, _...  49 us
    all_to_all x4, starting transfers between devices, sent(): lax.all_to_all(shaped, 'expert', 0, 0, tiled=True).reshape(2 * rows, half)  26.1 us
    dot_general x10, matrix products, dot(): lax.dot_general(left, right, (dims, ((), ())), preferred_element_type=jnp...  24.2 us
    all_to_all x4, waiting for transfers between devices, sent(): lax.all_to_all(shaped, 'expert', 0, 0, tiled=True).reshape(2 * rows, half)  21.3 us
    all_to_all x1, blocking collectives, local(): lax.all_to_all(sums.reshape(group, ROWS, LANES), 'expert', 0, 0, tiled=True)  18.6 us
    ppermute x4, waiting for transfers between devices, swapped(): return lax.ppermute(value, 'tensor', [(0, 1), (1, 0)])  16.6 us
    all_to_all x2, starting transfers between devices, from_everyone(): lax.all_to_all(jnp.broadcast_to(shard[None], (devices, *shard.shape)), ax...  10.1 us
    ppermute x4, starting transfers between devices, swapped(): return lax.ppermute(value, 'tensor', [(0, 1), (1, 0)])  9.15 us
  transfers between devices with their start and end apart: 18, of which 6 were waited for; matrix products, arithmetic and copies ran while one was open for 16% of the time, Pallas kernels for 19%

profile of v4, /device:TPU:1, one launch (start us, length us, event | category | flops | bytes accessed | tf_op | source)
XLA Modules:
  0.0 210.1 jit_solution(13413652733856629578)
XLA Ops:
  0.6 10.1 %shard_map.101 = (bf16[384,640]{1,0:T(8,128)(2,1)}, bf16[192,1280]{1,0:T(8,128)(2,1)}, bf16[6,256,1280]{2,1,0:T(8,128)(2,1)}, f32[6,256,128]{2,1,0:T(8,128)}, f3...) custom-call(bf16[6,256,1280]{2,1,0:T(8,128)(2,1)} %refs_0_.2, f32[1280]{0:T(1024)} %refs_1_.2, ...), custom_call_target="tpu_custom_call" | custom-call | flops 2516582400 | bytes 7864320 | tf_op jit(solution)/shard_map/pallas_call | solution.py:43
  10.8 10.0 %all-to-all-start.1 = ((bf16[16,24,640]{2,1,0:T(8,128)(2,1)}), bf16[16,24,640]{2,1,0:T(8,128)(2,1)}, u32[]{:S(2)}, u32[]{:S(2)}) async-start(bf16[16,24,640]{2,1,0:T(8,128)(2,1)} %bitcast.98), calls=%async_computation.1 | async-start | bytes 983040 | tf_op jit(solution)/shard_map/all_to_all | solution.py:444
  20.7 5.7 %shard_map.102 = bf16[384,640]{1,0:T(8,128)(2,1)} custom-call(bf16[6,256,1280]{2,1,0:T(8,128)(2,1)} %cot.1, f32[6,32,256]{2,1,0:T(8,128)} %get-tuple-element.33.refs_1_.refs_2_), custom_call_target="tpu_custom_call" | custom-call | flops 1258291200 | bytes 3932160 | tf_op jit(solution)/shard_map/pallas_call | solution.py:43
  26.4 11.0 %all-to-all-done.1 = bf16[16,24,640]{2,1,0:T(8,128)(2,1)} async-done(((bf16[16,24,640]{2,1,0:T(8,128)(2,1)}), bf16[16,24,640]{2,1,0:T(8,128)(2,1)}, u32[]{:S(2)}, u32[]{:S(2)}) %all-to-all-start.1) | async-done | bytes 491552 | tf_op jit(solution)/shard_map/all_to_all | solution.py:444
  37.4 4.1 %all-to-all-start = ((bf16[16,24,640]{2,1,0:T(8,128)(2,1)}), bf16[16,24,640]{2,1,0:T(8,128)(2,1)}, u32[]{:S(2)}, u32[]{:S(2)}) async-start(bf16[16,24,640]{2,1,0:T(8,128)(2,1)} %bitcast.97), calls=%async_computation | async-start | bytes 983040 | tf_op jit(solution)/shard_map/all_to_all | solution.py:444
  41.5 2.3 %shard_map.104 = bf16[192,1280]{1,0:T(8,128)(2,1)} custom-call(bf16[384,640]{1,0:T(8,128)(2,1)} %bitcast.5.refs_0_), custom_call_target="tpu_custom_call" | custom-call | flops 503316480 | bytes 983040 | tf_op jit(solution)/shard_map/pallas_call | solution.py:43
  43.8 2.9 %collective-permute-start.1 = (bf16[192,1280]{1,0:T(8,128)(2,1)}, bf16[192,1280]{1,0:T(8,128)(2,1)}, u32[]{:S(2)}, u32[]{:S(2)}) collective-permute-start(bf16[192,1280]{1,0:T(8,128)(2,1)} %shard_map.104), channel_id=1, source_target_pairs={{0,1},{1,0},{2,3},{3,2},{4,5},{5,4},{6,7},{7,6},{8,9},{9,8},{10,11... | collective-permute-start | bytes 1474568 | tf_op jit(solution)/shard_map/ppermute | solution.py:38
  46.7 10.3 %all-to-all-done = bf16[16,24,640]{2,1,0:T(8,128)(2,1)} async-done(((bf16[16,24,640]{2,1,0:T(8,128)(2,1)}), bf16[16,24,640]{2,1,0:T(8,128)(2,1)}, u32[]{:S(2)}, u32[]{:S(2)}) %all-to-all-start) | async-done | bytes 491552 | tf_op jit(solution)/shard_map/all_to_all | solution.py:444
  57.0 2.3 %shard_map.103 = bf16[192,1280]{1,0:T(8,128)(2,1)} custom-call(bf16[384,640]{1,0:T(8,128)(2,1)} %bitcast.2.refs_0_), custom_call_target="tpu_custom_call" | custom-call | flops 503316480 | bytes 983040 | tf_op jit(solution)/shard_map/pallas_call | solution.py:43
  59.3 2.9 %collective-permute-start = (bf16[192,1280]{1,0:T(8,128)(2,1)}, bf16[192,1280]{1,0:T(8,128)(2,1)}, u32[]{:S(2)}, u32[]{:S(2)}) collective-permute-start(bf16[192,1280]{1,0:T(8,128)(2,1)} %shard_map.103), channel_id=1, source_target_pairs={{0,1},{1,0},{2,3},{3,2},{4,5},{5,4},{6,7},{7,6},{8,9},{9,8},{10,11... | collective-permute-start | bytes 1474568 | tf_op jit(solution)/shard_map/ppermute | solution.py:38
  64.2 3.0 %multiply_convert_fusion = (bf16[192,1280]{1,0:T(8,128)(2,1)S(1)}, f32[192,1280]{1,0:T(8,128)}) fusion(bf16[192,1280]{1,0:T(8,128)(2,1)} %collective-permute-done.1, bf16[1,1280,1280]{2,1,0:T(8,128)(2,1)S(1)} %copy-done), kind=kOutput, calls=%fused_computation.51 | convolution fusion | flops 631357440 | bytes 5242880 | tf_op jit(solution)/shard_map/dot_general | solution.py:22
  69.2 3.2 %fusion.28 = bf16[192,1280]{1,0:T(8,128)(2,1)} fusion(f32[192,1280]{1,0:T(8,128)S(1)} %get-tuple-element.61, bf16[192,1280]{1,0:T(8,128)(2,1)} %shard_map.103, bf16[1,1280,1280]{2,1,0:T(8,128)(2,1)S(1)} %copy-done.3), kind=kOutput, calls=%fused_computation.31 | convolution fusion | flops 634060800 | bytes 5242880 | tf_op jit(solution)/shard_map/dot_general | solution.py:22
  72.5 11.4 %collective-permute-done.3.refs_1_ = bf16[192,1280]{1,0:T(8,128)(2,1)S(1)} collective-permute-done((bf16[192,1280]{1,0:T(8,128)(2,1)S(1)}, bf16[192,1280]{1,0:T(8,128)(2,1)S(1)}, u32[]{:S(2)}, u32[]{:S(2)}) %collective-permute-start.3) | collective-permute-done | bytes 491552 | tf_op jit(solution)/shard_map/ppermute | solution.py:38
  85.3 4.1 %all-to-all-start.3 = ((bf16[16,24,640]{2,1,0:T(8,128)(2,1)}), bf16[16,24,640]{2,1,0:T(8,128)(2,1)}, u32[]{:S(2)}, u32[]{:S(2)}) async-start(bf16[16,24,640]{2,1,0:T(8,128)(2,1)} %bitcast.88), calls=%async_computation.3 | async-start | bytes 983040 | tf_op jit(solution)/shard_map/all_to_all | solution.py:444
  89.4 3.7 %fusion.35 = bf16[192,1280]{1,0:T(8,128)(2,1)S(1)} fusion(f32[192,1280]{1,0:T(8,128)} %get-tuple-element.63, bf16[192,1280]{1,0:T(8,128)(2,1)} %collective-permute-done, bf16[1,1280,1280]{2,1,0:T(8,128)(2,1)} %param.11), kind=kOutput, calls=%fused_computation.38 | convolution fusion | flops 634060800 | bytes 5242880 | tf_op jit(solution)/shard_map/dot_general | solution.py:22
  94.4 3.0 %collective-permute-start.2 = (bf16[192,1280]{1,0:T(8,128)(2,1)S(1)}, bf16[192,1280]{1,0:T(8,128)(2,1)S(1)}, u32[]{:S(2)}, u32[]{:S(2)}) collective-permute-start(bf16[192,1280]{1,0:T(8,128)(2,1)S(1)} %fusion.19), channel_id=1, source_target_pairs={{0,1},{1,0},{2,3},{3,2},{4,5},{5,4},{6,7},{7,6},{8,9},{9,8},{10,11... | collective-permute-start | bytes 1474568 | tf_op jit(solution)/shard_map/ppermute | solution.py:38
  98.6 4.8 %convolution_convert_fusion.1 = bf16[1280,1280]{1,0:T(8,128)(2,1)} fusion(bf16[192,1280]{1,0:T(8,128)(2,1)} %collective-permute-done.1, bf16[192,1280]{1,0:T(8,128)(2,1)} %shard_map.104, bf16[192,1280]{1,0:T(8,128)(2,1)S(1)} %fusion.35, bf16[192,1280]{1,0:T(8,128)(2,1)S(1)} %copy-done.6), kind=kOutput, calls=%fused_computation.1 | convolution fusion | flops 1263861760 | bytes 5242880 | tf_op jit(solution)/shard_map/dot_general | solution.py:22
  103.4 5.1 %collective-permute-done.2.refs_1_ = bf16[192,1280]{1,0:T(8,128)(2,1)S(1)} collective-permute-done((bf16[192,1280]{1,0:T(8,128)(2,1)S(1)}, bf16[192,1280]{1,0:T(8,128)(2,1)S(1)}, u32[]{:S(2)}, u32[]{:S(2)}) %collective-permute-start.2) | collective-permute-done | bytes 491552 | tf_op jit(solution)/shard_map/ppermute | solution.py:38
  110.0 7.9 %all-to-all-start.2 = ((bf16[16,24,640]{2,1,0:T(8,128)(2,1)}), bf16[16,24,640]{2,1,0:T(8,128)(2,1)}, u32[]{:S(2)}, u32[]{:S(2)}) async-start(bf16[16,24,640]{2,1,0:T(8,128)(2,1)} %bitcast.87), calls=%async_computation.2 | async-start | bytes 983040 | tf_op jit(solution)/shard_map/all_to_all | solution.py:444
  117.8 2.7 %dynamic-slice_bitcast_fusion = bf16[4,160,1280]{2,1,0:T(8,128)(2,1)} fusion(bf16[4,2,160,1280]{3,2,1,0:T(8,128)(2,1)} %bitcast.91, s32[]{:T(128)S(6)} %select_n.45), kind=kLoop, calls=%fused_computation.20 | loop fusion | bytes 3276804 | tf_op jit(solution)/shard_map/jit(dynamic_index_in_dim)/squeeze | solution.py:334
  121.9 3.4 %convolution_convert_fusion = bf16[1280,1280]{1,0:T(8,128)(2,1)S(1)} fusion(bf16[192,1280]{1,0:T(8,128)(2,1)} %collective-permute-done, bf16[192,1280]{1,0:T(8,128)(2,1)} %shard_map.103, bf16[192,1280]{1,0:T(8,128)(2,1)} %copy-done.7, bf16[192,1280]{1,0:T(8,128)(2,1)} %copy-done.5), kind=kOutput, calls=%fused_computation | convolution fusion | flops 1263861760 | bytes 5242880 | tf_op jit(solution)/shard_map/dot_general | solution.py:22
  129.6 2.5 %collective-permute-start.9 = (bf16[320,1280]{1,0:T(8,128)(2,1)}, bf16[320,1280]{1,0:T(8,128)(2,1)}, u32[]{:S(2)}, u32[]{:S(2)}) collective-permute-start(bf16[320,1280]{1,0:T(8,128)(2,1)} %get-tuple-element.58), channel_id=1, source_target_pairs={{0,128},{32,160},{64,192},{96,224},{128,0},{160,32},{192,64},{224,... | collective-permute-start | bytes 2457608 | tf_op jit(solution)/shard_map/ppermute | solution.py:411
  133.8 4.5 %shard_map.107.refs_5_ = f32[6,32,256]{2,1,0:T(8,128)} custom-call(bf16[384,640]{1,0:T(8,128)(2,1)} %bitcast.10.refs_0_, bf16[6,256,1280]{2,1,0:T(8,128)(2,1)} %cot.1, f32[6,32,256]{2,1,0:T(8,128)} %get-tuple-element.33.refs_1_.refs_2_), custom_call_target="tpu_custom_call" | custom-call | flops 1258291200 | bytes 3932160 | tf_op jit(solution)/shard_map/pallas_call | solution.py:43
  138.4 5.5 %shard_map.108 = (bf16[192,1280]{1,0:T(8,128)(2,1)}, bf16[6,80,256]{2,1,0:T(8,128)(2,1)}, f32[384,128]{1,0:T(8,128)}) custom-call(bf16[384,640]{1,0:T(8,128)(2,1)} %bitcast.8.refs_0_, bf16[192,1280]{1,0:T(8,128)(2,1)} %get-tuple-element.35.refs_1_, bf16[6,256,1280]{2,1,0:T(8,128)(2,1)} %get-tuple-element.31.refs_2_.normed, ...), custom_call_target="tpu_custom_call" | custom-call | flops 1887436800 | bytes 3932160 | tf_op jit(solution)/shard_map/pallas_call | solution.py:43
  143.9 18.6 %all_to_all.35 = f32[16,24,128]{2,1,0:T(8,128)S(1)} all-to-all(f32[16,24,128]{2,1,0:T(8,128)} %bitcast.102), channel_id=1, replica_groups=mesh['dp'=8,'expert'=16,'tensor'=2] {'expert'}, dimensions={0} | all-to-all | bytes 393216 | tf_op jit(solution)/shard_map/all_to_all | solution.py:586
  163.1 4.0 %all-to-all-start.5 = ((f32[16,24,128]{2,1,0:T(8,128)}), f32[16,24,128]{2,1,0:T(8,128)S(1)}, u32[]{:S(2)}, u32[]{:S(2)}) async-start(f32[16,24,128]{2,1,0:T(8,128)} %broadcast_in_dim.8), calls=%async_computation.5 | async-start | bytes 393216 | tf_op jit(solution)/shard_map/all_to_all | solution.py:32
  167.8 3.8 %shard_map.111 = (f32[160,1280]{1,0:T(8,128)}, bf16[160,1280]{1,0:T(8,128)(2,1)}) custom-call(s32[2]{0:T(128)} %pad_add_fusion.where, bf16[4,320,1280]{2,1,0:T(8,128)(2,1)} %bitcast.90, bf16[320,1280]{1,0:T(8,128)(2,1)} %collective-permute-done.8.refs_0_, bf16[320,1280]{1,0:T(8,128)(2,1)} %collective-permute-done.9.refs_1_, ...), custom_call_target="tpu_custom_call" | custom-call | flops 163840000 | bytes 3276800 | tf_op jit(solution)/shard_map/pallas_call | solution.py:43
  175.6 6.1 %all-to-all-start.6 = ((f32[16,24,128]{2,1,0:T(8,128)}), f32[16,24,128]{2,1,0:T(8,128)S(1)}, u32[]{:S(2)}, u32[]{:S(2)}) async-start(f32[16,24,128]{2,1,0:T(8,128)} %broadcast_in_dim.9), calls=%async_computation.6 | async-start | bytes 393216 | tf_op jit(solution)/shard_map/all_to_all | solution.py:32
  181.7 3.8 %shard_map.110 = (bf16[160,1280]{1,0:T(8,128)(2,1)}, bf16[160,1280]{1,0:T(8,128)(2,1)}, bf16[160,1280]{1,0:T(8,128)(2,1)}, bf16[160,1280]{1,0:T(8,128)(2,1)}) custom-call(s32[2]{0:T(128)} %pad_add_fusion.where, bf16[4,2,160,1280]{3,2,1,0:T(8,128)(2,1)} %bitcast.92, bf16[4,160,1280]{2,1,0:T(8,128)(2,1)} %collective-permute-done.4.far_other), custom_call_target="tpu_custom_call" | custom-call | flops 81920000 | bytes 4915200 | tf_op jit(solution)/shard_map/pallas_call | solution.py:43
  190.4 9.9 %shard_map.109 = bf16[6,256,1280]{2,1,0:T(8,128)(2,1)} custom-call(bf16[6,256,1280]{2,1,0:T(8,128)(2,1)} %get-tuple-element.31.refs_2_.normed, bf16[6,256,1280]{2,1,0:T(8,128)(2,1)} %cot.1, f32[6,256,128]{2,1,0:T(8,128)} %get-tuple-element.32.inverse, bf16[6,80,256]{2,1,0:T(8,128)(2,1)} %get-tuple-element.38.pair, ...), custom_call_target="tpu_custom_call" | custom-call | flops 2516582400 | bytes 11796480 | tf_op jit(solution)/shard_map/pallas_call | solution.py:43
  202.4 4.9 %collective-permute-done.6 = bf16[160,1280]{1,0:T(8,128)(2,1)} collective-permute-done((bf16[160,1280]{1,0:T(8,128)(2,1)}, bf16[160,1280]{1,0:T(8,128)(2,1)}, u32[]{:S(2)}, u32[]{:S(2)}) %collective-permute-start.6) | collective-permute-done | bytes 409632 | tf_op jit(solution)/shard_map/ppermute | solution.py:593
  207.2 2.9 %fusion.52 = (bf16[1,160,1280]{2,1,0:T(8,128)(2,1)}, bf16[1,1280,160]{1,2,0:T(8,128)(2,1)}) fusion(bf16[160,1280]{1,0:T(8,128)(2,1)} %collective-permute-done.7, bf16[160,1280]{1,0:T(8,128)(2,1)} %collective-permute-done.6, bf16[160,1280]{1,0:T(8,128)(2,1)} %collective-permute-done.5, bf16[160,1280]{1,0:T(8,128)(2,1)} %get-tuple-element.47, ...), kind=kLoop, calls=%fused_computation.58 | loop fusion | flops 2252800 | bytes 3686400 | tf_op jit(solution)/shard_map/broadcast_in_dim | solution.py:633
  (59 shorter events, 28.8 us)
Async XLA Ops:
  0.6 61.6 %copy-start = (bf16[1,1280,1280]{2,1,0:T(8,128)(2,1)S(1)}, bf16[1,1280,1280]{2,1,0:T(8,128)(2,1)}, u32[]{:S(2)}) copy-start(bf16[1,1280,1280]{2,1,0:T(8,128)(2,1)} %param.10) | copy-start | bytes 9830404
  10.8 26.6 %all-to-all-start.1 = ((bf16[16,24,640]{2,1,0:T(8,128)(2,1)}), bf16[16,24,640]{2,1,0:T(8,128)(2,1)}, u32[]{:S(2)}, u32[]{:S(2)}) async-start(bf16[16,24,640]{2,1,0:T(8,128)(2,1)} %bitcast.98), calls=%async_computation.1 | async-start | bytes 983040 | tf_op jit(solution)/shard_map/all_to_all | solution.py:444
  37.4 19.7 %all-to-all-start = ((bf16[16,24,640]{2,1,0:T(8,128)(2,1)}), bf16[16,24,640]{2,1,0:T(8,128)(2,1)}, u32[]{:S(2)}, u32[]{:S(2)}) async-start(bf16[16,24,640]{2,1,0:T(8,128)(2,1)} %bitcast.97), calls=%async_computation | async-start | bytes 983040 | tf_op jit(solution)/shard_map/all_to_all | solution.py:444
  43.8 20.4 %collective-permute-start.1 = (bf16[192,1280]{1,0:T(8,128)(2,1)}, bf16[192,1280]{1,0:T(8,128)(2,1)}, u32[]{:S(2)}, u32[]{:S(2)}) collective-permute-start(bf16[192,1280]{1,0:T(8,128)(2,1)} %shard_map.104), channel_id=1, source_target_pairs={{0,1},{1,0},{2,3},{3,2},{4,5},{5,4},{6,7},{7,6},{8,9},{9,8},{10,11... | collective-permute-start | bytes 1474568 | tf_op jit(solution)/shard_map/ppermute | solution.py:38
  59.3 30.1 %collective-permute-start = (bf16[192,1280]{1,0:T(8,128)(2,1)}, bf16[192,1280]{1,0:T(8,128)(2,1)}, u32[]{:S(2)}, u32[]{:S(2)}) collective-permute-start(bf16[192,1280]{1,0:T(8,128)(2,1)} %shard_map.103), channel_id=1, source_target_pairs={{0,1},{1,0},{2,3},{3,2},{4,5},{5,4},{6,7},{7,6},{8,9},{9,8},{10,11... | collective-permute-start | bytes 1474568 | tf_op jit(solution)/shard_map/ppermute | solution.py:38
  64.1 4.2 %copy-start.5 = (bf16[192,1280]{1,0:T(8,128)(2,1)}, bf16[192,1280]{1,0:T(8,128)(2,1)S(1)}, u32[]{:S(2)}) copy-start(bf16[192,1280]{1,0:T(8,128)(2,1)S(1)} %get-tuple-element.60) | copy-start | bytes 1474564
  64.2 3.1 %copy-start.3 = (bf16[1,1280,1280]{2,1,0:T(8,128)(2,1)S(1)}, bf16[1,1280,1280]{2,1,0:T(8,128)(2,1)}, u32[]{:S(2)}) copy-start(bf16[1,1280,1280]{2,1,0:T(8,128)(2,1)} %param.11) | copy-start | bytes 9830404
  67.2 2.0 copy-start.7
  68.1 15.8 %collective-permute-start.3 = (bf16[192,1280]{1,0:T(8,128)(2,1)S(1)}, bf16[192,1280]{1,0:T(8,128)(2,1)S(1)}, u32[]{:S(2)}, u32[]{:S(2)}) collective-permute-start(bf16[192,1280]{1,0:T(8,128)(2,1)S(1)} %fusion.16), channel_id=1, source_target_pairs={{0,1},{1,0},{2,3},{3,2},{4,5},{5,4},{6,7},{7,6},{8,9},{9,8},{10,11... | collective-permute-start | bytes 1474568 | tf_op jit(solution)/shard_map/ppermute | solution.py:38
  84.5 0.8 copy-start.2
  85.3 24.7 %all-to-all-start.3 = ((bf16[16,24,640]{2,1,0:T(8,128)(2,1)}), bf16[16,24,640]{2,1,0:T(8,128)(2,1)}, u32[]{:S(2)}, u32[]{:S(2)}) async-start(bf16[16,24,640]{2,1,0:T(8,128)(2,1)} %bitcast.88), calls=%async_computation.3 | async-start | bytes 983040 | tf_op jit(solution)/shard_map/all_to_all | solution.py:444
  93.2 4.2 %copy-start.6 = (bf16[192,1280]{1,0:T(8,128)(2,1)S(1)}, bf16[192,1280]{1,0:T(8,128)(2,1)}, u32[]{:S(2)}) copy-start(bf16[192,1280]{1,0:T(8,128)(2,1)} %fusion.28) | copy-start | bytes 1474564
  94.4 14.2 %collective-permute-start.2 = (bf16[192,1280]{1,0:T(8,128)(2,1)S(1)}, bf16[192,1280]{1,0:T(8,128)(2,1)S(1)}, u32[]{:S(2)}, u32[]{:S(2)}) collective-permute-start(bf16[192,1280]{1,0:T(8,128)(2,1)S(1)} %fusion.19), channel_id=1, source_target_pairs={{0,1},{1,0},{2,3},{3,2},{4,5},{5,4},{6,7},{7,6},{8,9},{9,8},{10,11... | collective-permute-start | bytes 1474568 | tf_op jit(solution)/shard_map/ppermute | solution.py:38
  109.2 0.8 copy-start.1
  110.0 28.4 %all-to-all-start.2 = ((bf16[16,24,640]{2,1,0:T(8,128)(2,1)}), bf16[16,24,640]{2,1,0:T(8,128)(2,1)}, u32[]{:S(2)}, u32[]{:S(2)}) async-start(bf16[16,24,640]{2,1,0:T(8,128)(2,1)} %bitcast.87), calls=%async_computation.2 | async-start | bytes 983040 | tf_op jit(solution)/shard_map/all_to_all | solution.py:444
  120.6 61.2 %collective-permute-start.4 = (bf16[4,160,1280]{2,1,0:T(8,128)(2,1)}, bf16[4,160,1280]{2,1,0:T(8,128)(2,1)}, u32[]{:S(2)}, u32[]{:S(2)}) collective-permute-start(bf16[4,160,1280]{2,1,0:T(8,128)(2,1)} %dynamic-slice_bitcast_fusion), channel_id=1, source_target_pairs={{0,32},{32,0},{64,96},{96,64},{128,160},{160,128},{192,224},{224,1... | collective-permute-start | bytes 4915208 | tf_op jit(solution)/shard_map/ppermute | solution.py:418
  125.2 1.7 copy-start.4
  125.2 8.0 %copy-start.9 = (f32[1280]{0:T(1024)S(1)}, f32[1280]{0:T(1024)}, u32[]{:S(2)}) copy-start(f32[1280]{0:T(1024)} %refs_1_.2) | copy-start | bytes 15364
  128.4 39.4 %collective-permute-start.8 = (bf16[320,1280]{1,0:T(8,128)(2,1)}, bf16[320,1280]{1,0:T(8,128)(2,1)}, u32[]{:S(2)}, u32[]{:S(2)}) collective-permute-start(bf16[320,1280]{1,0:T(8,128)(2,1)} %get-tuple-element.59), channel_id=1, source_target_pairs={{0,64},{32,96},{64,128},{96,160},{128,192},{160,224},{192,0},{224,... | collective-permute-start | bytes 2457608 | tf_op jit(solution)/shard_map/ppermute | solution.py:411
  129.6 38.2 %collective-permute-start.9 = (bf16[320,1280]{1,0:T(8,128)(2,1)}, bf16[320,1280]{1,0:T(8,128)(2,1)}, u32[]{:S(2)}, u32[]{:S(2)}) collective-permute-start(bf16[320,1280]{1,0:T(8,128)(2,1)} %get-tuple-element.58), channel_id=1, source_target_pairs={{0,128},{32,160},{64,192},{96,224},{128,0},{160,32},{192,64},{224,... | collective-permute-start | bytes 2457608 | tf_op jit(solution)/shard_map/ppermute | solution.py:411
  132.1 35.8 %collective-permute-start.10 = (bf16[320,1280]{1,0:T(8,128)(2,1)}, bf16[320,1280]{1,0:T(8,128)(2,1)}, u32[]{:S(2)}, u32[]{:S(2)}) collective-permute-start(bf16[320,1280]{1,0:T(8,128)(2,1)} %get-tuple-element.57), channel_id=1, source_target_pairs={{0,192},{32,224},{64,0},{96,32},{128,64},{160,96},{192,128},{224,1... | collective-permute-start | bytes 2457608 | tf_op jit(solution)/shard_map/ppermute | solution.py:411
  163.1 11.8 %all-to-all-start.5 = ((f32[16,24,128]{2,1,0:T(8,128)}), f32[16,24,128]{2,1,0:T(8,128)S(1)}, u32[]{:S(2)}, u32[]{:S(2)}) async-start(f32[16,24,128]{2,1,0:T(8,128)} %broadcast_in_dim.8), calls=%async_computation.5 | async-start | bytes 393216 | tf_op jit(solution)/shard_map/all_to_all | solution.py:32
  171.7 28.6 %collective-permute-start.11 = (bf16[160,1280]{1,0:T(8,128)(2,1)}, bf16[160,1280]{1,0:T(8,128)(2,1)}, u32[]{:S(2)}, u32[]{:S(2)}) collective-permute-start(bf16[160,1280]{1,0:T(8,128)(2,1)} %get-tuple-element.55), channel_id=1, source_target_pairs={{0,32},{32,0},{64,96},{96,64},{128,160},{160,128},{192,224},{224,1... | collective-permute-start | bytes 1228808 | tf_op jit(solution)/shard_map/ppermute | solution.py:418
  175.6 24.7 %all-to-all-start.6 = ((f32[16,24,128]{2,1,0:T(8,128)}), f32[16,24,128]{2,1,0:T(8,128)S(1)}, u32[]{:S(2)}, u32[]{:S(2)}) async-start(f32[16,24,128]{2,1,0:T(8,128)} %broadcast_in_dim.9), calls=%async_computation.6 | async-start | bytes 393216 | tf_op jit(solution)/shard_map/all_to_all | solution.py:32
  185.5 16.8 %collective-permute-start.5 = (bf16[160,1280]{1,0:T(8,128)(2,1)}, bf16[160,1280]{1,0:T(8,128)(2,1)}, u32[]{:S(2)}, u32[]{:S(2)}) collective-permute-start(bf16[160,1280]{1,0:T(8,128)(2,1)} %get-tuple-element.44), channel_id=1, source_target_pairs={{0,64},{32,96},{64,128},{96,160},{128,192},{160,224},{192,0},{224,... | collective-permute-start | bytes 1228808 | tf_op jit(solution)/shard_map/ppermute | solution.py:593
  187.0 20.2 %collective-permute-start.6 = (bf16[160,1280]{1,0:T(8,128)(2,1)}, bf16[160,1280]{1,0:T(8,128)(2,1)}, u32[]{:S(2)}, u32[]{:S(2)}) collective-permute-start(bf16[160,1280]{1,0:T(8,128)(2,1)} %get-tuple-element.45), channel_id=1, source_target_pairs={{0,128},{32,160},{64,192},{96,224},{128,0},{160,32},{192,64},{224,... | collective-permute-start | bytes 1228808 | tf_op jit(solution)/shard_map/ppermute | solution.py:593
  188.7 18.6 %collective-permute-start.7 = (bf16[160,1280]{1,0:T(8,128)(2,1)}, bf16[160,1280]{1,0:T(8,128)(2,1)}, u32[]{:S(2)}, u32[]{:S(2)}) collective-permute-start(bf16[160,1280]{1,0:T(8,128)(2,1)} %get-tuple-element.46), channel_id=1, source_target_pairs={{0,192},{32,224},{64,0},{96,32},{128,64},{160,96},{192,128},{224,1... | collective-permute-start | bytes 1228808 | tf_op jit(solution)/shard_map/ppermute | solution.py:593
  190.4 10.6 %copy-start.8 = (bf16[1280,32]{0,1:T(8,128)(2,1)S(1)}, bf16[1280,32]{0,1:T(8,128)(2,1)}, u32[]{:S(2)}) copy-start(bf16[1280,32]{0,1:T(8,128)(2,1)} %param.9) | copy-start | bytes 245764
